TPU v7x, 256 devices: a whole 4x4x8 slice. The times are simulated.
256 devices in a mesh: lat: 64 (over x_lo, z, y), dp: 4 (over x_hi, core).
Axes of the slice: x: 4 (x_hi: 2, x_lo: 2; x = x_hi * 2 + x_lo), y: 4, z: 8, core: 2. Of those that a mesh axis runs over, the one named last changes fastest.
Arguments:
- state: float32 [4, 128, 256, 128], P('dp', 'lat'), may hold values from -6 to 6
- cotangent: float32 [4, 128, 256, 128], P('dp', 'lat'), may hold values from -0.18 to 0.18
- w_first: bfloat16 [128, 1024], replicated, may hold values from -0.5 to 0.5
- w_middle: bfloat16 [1024, 1024], replicated, may hold values from -0.1875 to 0.1875
- w_last: bfloat16 [1024, 128], replicated, may hold values from -0.1875 to 0.1875
Outputs:
- final_state: float32 [4, 128, 256, 128], P('dp', 'lat')
- grad_first: float32 [128, 1024], replicated
- grad_middle: float32 [1024, 1024], replicated
- grad_last: float32 [1024, 128], replicated
All inputs are finite; a program needn't handle non-finite values.
Results may differ from a plain program's by a relative error of at most 0.0048.
Values sent between devices are 32-bit elements; how exact they have to be, the bound alone decides.
A program may use at most 64 MiB of HBM per device.

v0:
```python
import math

import jax
import jax.numpy as jnp
from jax import lax
from jax.sharding import PartitionSpec as P

MW = 64
STEPS = 2


highest = lax.Precision.HIGHEST
tend_weight = 0.5


def grid_tables(lon_count, wave_count):
    lon_index = jnp.arange(lon_count, dtype=jnp.int32)
    wave_index = jnp.arange(wave_count, dtype=jnp.int32)
    phase_angle = (lon_index[:, None] * wave_index[None, :] % lon_count).astype(jnp.float32) * (
        2.0 * math.pi / lon_count
    )
    cosine = jnp.cos(phase_angle)
    sine_part = jnp.sin(phase_angle)
    analysis = jnp.stack([cosine, -sine_part], axis=2) / lon_count
    factor = jnp.where(wave_index == 0, 1.0, 2.0).astype(jnp.float32)
    synthesis = jnp.stack([cosine, -sine_part], axis=2) * factor[None, :, None]
    return (analysis, synthesis)


def legendre(wave_ids, lat_count, wave_count):
    lat_index = jnp.arange(lat_count).astype(jnp.float32)
    latitude = (lat_index + 0.5) * (math.pi / lat_count) - 0.5 * math.pi
    sine_lat = jnp.sin(latitude)
    cosine_lat = jnp.cos(latitude)
    quad_weight = cosine_lat * (math.pi / lat_count)
    order_m = wave_ids.astype(jnp.float32)
    counter = jnp.arange(1, wave_count).astype(jnp.float32)
    increments = 0.5 * jnp.log((2.0 * counter + 1.0) / (2.0 * counter))
    summed = jnp.sum(
        jnp.where(counter[None, :] <= order_m[:, None], increments[None, :], 0.0), axis=1
    )
    diagonal = jnp.exp(
        0.5 * math.log(0.5) + summed[:, None] + order_m[:, None] * jnp.log(cosine_lat)[None, :]
    )

    def advance(carry, offset):
        previous, current, ratio_prev = carry
        degree = order_m + offset
        ratio_new = jnp.sqrt((4.0 * degree * degree - 1.0) / (degree * degree - order_m * order_m))
        following = ratio_new[:, None] * (
            sine_lat[None, :] * current - previous / ratio_prev[:, None]
        )
        return ((current, following, ratio_new), following)

    initial = (jnp.zeros_like(diagonal), diagonal, jnp.ones_like(order_m))
    _, remaining = lax.scan(advance, initial, jnp.arange(1, wave_count).astype(jnp.float32))
    poly_table = jnp.concatenate([diagonal[None], remaining], axis=0).transpose(1, 0, 2)
    degree = order_m[:, None] + jnp.arange(wave_count).astype(jnp.float32)[None, :]
    kept_mask = degree <= wave_count - 1
    poly_table = jnp.where(kept_mask[:, :, None], poly_table, 0.0)
    damping = jnp.where(
        kept_mask, 1.0 / (1.0 + degree * (degree + 1.0) / (wave_count * (wave_count - 1.0))), 0.0
    )
    return (poly_table, quad_weight, damping)


def silu_slope(value):
    gate_sig = jax.nn.sigmoid(value)
    return gate_sig * (1.0 + value * (1.0 - gate_sig))


def hidden_rows(rows, w_first, w_middle):
    pre_first = jnp.dot(rows, w_first, preferred_element_type=jnp.float32)
    hidden_first = jax.nn.silu(pre_first).astype(jnp.bfloat16)
    pre_middle = jnp.dot(hidden_first, w_middle, preferred_element_type=jnp.float32)
    hidden_middle = jax.nn.silu(pre_middle).astype(jnp.bfloat16)
    return (pre_first, hidden_first, pre_middle, hidden_middle)


def body(state, cotangent, w_first, w_middle, w_last):
    sample, lat_rows, lon_count, features = state.shape
    hidden_count = w_first.shape[1]
    band_count = lax.axis_size("lat")
    lat_count = lat_rows * band_count
    local_waves = MW // band_count
    wave_ids = lax.axis_index("lat") * local_waves + jnp.arange(local_waves, dtype=jnp.int32)
    analysis, synthesis = grid_tables(lon_count, MW)
    poly_table, quad_weight, damping = legendre(wave_ids, lat_count, MW)
    weighted = poly_table * quad_weight[None, None, :]
    row_count = sample * lat_rows * lon_count

    def spectral(field, first, last, in_table, out_table):
        wave_grid = jnp.einsum("bjxf,xmp->bjmpf", field, first, precision=highest)
        coeffs = (
            jnp.einsum(
                "mkj,bjmpf->bmkpf",
                in_table,
                lax.all_to_all(wave_grid, "lat", split_axis=2, concat_axis=1, tiled=True),
                precision=highest,
            )
            * damping[None, :, :, None, None]
        )
        back_grid = jnp.einsum("mkj,bmkpf->bjmpf", out_table, coeffs, precision=highest)
        back_bands = lax.all_to_all(back_grid, "lat", split_axis=1, concat_axis=2, tiled=True)
        return jnp.einsum("bjmpf,xmp->bjxf", back_bands, last, precision=highest)

    saved = []
    field = state
    for step_index in range(STEPS):
        rows = field.reshape(row_count, features).astype(jnp.bfloat16)
        pre_first, hidden_first, pre_middle, hidden_middle = hidden_rows(rows, w_first, w_middle)
        tendency = jnp.dot(hidden_middle, w_last, preferred_element_type=jnp.float32)
        saved.append((rows, pre_first, hidden_first, pre_middle, hidden_middle))
        moved = field + tend_weight * tendency.reshape(field.shape)
        field = spectral(moved, analysis, synthesis, weighted, poly_table)
    grad = cotangent
    total_first = jnp.zeros((features, hidden_count), jnp.float32)
    total_middle = jnp.zeros((hidden_count, hidden_count), jnp.float32)
    total_last = jnp.zeros((hidden_count, features), jnp.float32)
    for step_index in reversed(range(STEPS)):
        pulled = spectral(grad, synthesis, analysis, poly_table, weighted)
        scaled = (tend_weight * pulled).astype(jnp.bfloat16).reshape(row_count, features)
        rows, pre_first, hidden_first, pre_middle, hidden_middle = saved[step_index]
        total_last = total_last + jnp.dot(
            hidden_middle.T, scaled, preferred_element_type=jnp.float32
        )
        middle_back = jnp.dot(scaled, w_last.T, preferred_element_type=jnp.float32)
        middle_grad = (middle_back * silu_slope(pre_middle)).astype(jnp.bfloat16)
        total_middle = total_middle + jnp.dot(
            hidden_first.T, middle_grad, preferred_element_type=jnp.float32
        )
        first_back = jnp.dot(middle_grad, w_middle.T, preferred_element_type=jnp.float32)
        first_grad = (first_back * silu_slope(pre_first)).astype(jnp.bfloat16)
        total_first = total_first + jnp.dot(rows.T, first_grad, preferred_element_type=jnp.float32)
        if step_index > 0:
            back_rows = jnp.dot(first_grad, w_first.T, preferred_element_type=jnp.float32)
            grad = pulled + back_rows.reshape(field.shape)
    total_first, total_middle, total_last = lax.psum(
        (total_first, total_middle, total_last), ("lat", "dp")
    )
    return (field, total_first, total_middle, total_last)


def solution(mesh):
    in_specs = (P("dp", "lat", None, None), P("dp", "lat", None, None), P(), P(), P())
    out_specs = (P("dp", "lat", None, None), P(), P(), P())
    return jax.shard_map(body, mesh=mesh, in_specs=in_specs, out_specs=out_specs, check_vma=False)
```

profile of v0, /device:TPU:1, one launch (start us, length us, event | category | flops | bytes accessed | tf_op | source)
XLA Modules:
  0.0 566.1 jit_solution(16079854312345815015)
XLA Ops:
  9.5 13.8 %all-to-all-start.4 = ((f32[1,2,64,2,128]{4,1,3,0,2:T(2,128)}), f32[1,2,64,2,128]{4,1,3,0,2:T(2,128)}, u32[]{:S(2)}, u32[]{:S(2)}) async-start(f32[1,2,64,2,128]{4,1,3,0,2:T(2,128)} %copy.40), calls=%async_computation.4 | async-start | bytes 262144 | tf_op jit(solution)/shard_map/all_to_all | solution.py:98
  24.9 125.0 %while.19 = (s32[]{:T(128)}, f32[1,128]{1,0:T(1,128)S(1)}, f32[1,128]{1,0:T(1,128)S(1)}, f32[1]{0:T(128)}, f32[63,1,128]{2,1,0:T(1,128)}, /*index=5*/f32[63]{0:T...) while((s32[]{:T(128)}, f32[1,128]{1,0:T(1,128)S(1)}, ...), condition=%wide.region_2.3_spmd.clone, body=%wide.region_1.2_spmd.clone.sunk | while | flops 1033 | bytes 5353 | solution.py:56
  152.0 2.8 multiply_convert_fusion.6
  157.8 10.9 %all-to-all-start = ((f32[1,2,64,2,128]{4,1,3,0,2:T(2,128)}), f32[1,2,64,2,128]{4,1,3,0,2:T(2,128)}, u32[]{:S(2)}, u32[]{:S(2)}) async-start(f32[1,2,64,2,128]{4,1,3,0,2:T(2,128)} %copy.29), calls=%async_computation | async-start | bytes 262144 | tf_op jit(solution)/shard_map/all_to_all | solution.py:98
  174.1 4.3 all-to-all-done
  178.5 6.6 %all-to-all-start.5 = ((f32[1,128,1,2,128]{4,3,0,2,1:T(2,128)}), f32[1,128,1,2,128]{4,3,0,2,1:T(2,128)}, u32[]{:S(2)}, u32[]{:S(2)}) async-start(f32[1,128,1,2,128]{4,3,0,2,1:T(2,128)} %copy.42), calls=%async_computation.5 | async-start | bytes 262144 | tf_op jit(solution)/shard_map/all_to_all | solution.py:104
  190.5 4.4 all-to-all-done.5
  194.9 6.7 %all-to-all-start.1 = ((f32[1,128,1,2,128]{4,3,0,2,1:T(2,128)}), f32[1,128,1,2,128]{4,3,0,2,1:T(2,128)}, u32[]{:S(2)}, u32[]{:S(2)}) async-start(f32[1,128,1,2,128]{4,3,0,2,1:T(2,128)} %copy.32), calls=%async_computation.1 | async-start | bytes 262144 | tf_op jit(solution)/shard_map/all_to_all | solution.py:104
  203.7 7.7 %all-to-all-done.1 = f32[1,128,1,2,128]{4,3,0,2,1:T(2,128)} async-done(((f32[1,128,1,2,128]{4,3,0,2,1:T(2,128)}), f32[1,128,1,2,128]{4,3,0,2,1:T(2,128)}, u32[]{:S(2)}, u32[]{:S(2)}) %all-to-all-start.1) | async-done | bytes 131104 | tf_op jit(solution)/shard_map/all_to_all | solution.py:104
  214.5 2.6 multiply_convert_fusion.4
  222.3 5.4 all-to-all-start.6
  227.7 5.2 fusion.93
  232.9 4.6 all-to-all-done.6
  243.0 6.4 %all-to-all-start.7 = ((f32[1,128,1,2,128]{4,3,0,2,1:T(2,128)}), f32[1,128,1,2,128]{4,3,0,2,1:T(2,128)}, u32[]{:S(2)}, u32[]{:S(2)}) async-start(f32[1,128,1,2,128]{4,3,0,2,1:T(2,128)} %copy.47), calls=%async_computation.7 | async-start | bytes 262144 | tf_op jit(solution)/shard_map/all_to_all | solution.py:104
  249.6 2.5 fusion.100
  252.1 7.0 %all-to-all-done.7 = f32[1,128,1,2,128]{4,3,0,2,1:T(2,128)} async-done(((f32[1,128,1,2,128]{4,3,0,2,1:T(2,128)}), f32[1,128,1,2,128]{4,3,0,2,1:T(2,128)}, u32[]{:S(2)}, u32[]{:S(2)}) %all-to-all-start.7) | async-done | bytes 131104 | tf_op jit(solution)/shard_map/all_to_all | solution.py:104
  260.5 3.5 multiply_convert_fusion.1
  265.3 4.6 fusion.4
  269.9 2.3 convolution_add_fusion.2
  272.2 5.9 %convolution_add_fusion = f32[1024,1024]{1,0:T(8,128)} fusion(f32[1024,1024]{1,0:T(8,128)} %fusion.93, bf16[512,1024]{1,0:T(8,128)(2,1)} %multiply_convert_fusion.1, f32[512,1024]{1,0:T(8,128)S(1)} %copy-done.7), kind=kOutput, calls=%fused_computation.5 | convolution fusion | flops 1077411840 | bytes 11534336 | tf_op jit(solution)/shard_map/dot_general | solution.py:129
  281.1 13.8 %all_to_all.120 = f32[1,2,64,2,128]{4,1,3,0,2:T(2,128)S(1)} all-to-all(f32[1,2,64,2,128]{4,1,3,0,2:T(2,128)S(1)} %copy.35), channel_id=1, replica_groups=mesh['lat'=64,'dp'=4] {'lat'}, dimensions={2} | all-to-all | bytes 262144 | tf_op jit(solution)/shard_map/all_to_all | solution.py:98
  295.7 14.1 %all_to_all.121 = f32[1,128,1,2,128]{4,3,0,2,1:T(2,128)S(1)} all-to-all(f32[1,128,1,2,128]{4,3,0,2,1:T(2,128)S(1)} %copy.37), channel_id=1, replica_groups=mesh['lat'=64,'dp'=4] {'lat'}, dimensions={1} | all-to-all | bytes 262144 | tf_op jit(solution)/shard_map/all_to_all | solution.py:104
  311.0 240.6 %all-reduce.3.cloned.1.call-done = (f32[128,1024]{1,0:T(8,128)}, f32[1024,1024]{1,0:T(8,128)}, f32[1024,128]{1,0:T(8,128)}) async-done(((f32[128,1024]{1,0:T(8,128)}, f32[1024,1024]{1,0:T(8,128)}, f32[1024,128]{1,0:T(8,128)}), (f32[128,1024]{1,0:T(8,128)}, f32[1024,1024]{1,0:T(8,128)}, f32[1024,128]{1,0:T(8,128)})) %all-reduce.3.cloned.1.call-update) | async-done | bytes 5242896 | tf_op jit(solution)/shard_map/psum | solution.py:138
  553.6 4.8 copy.110
  (358 shorter events, 121.9 us)
Async XLA Ops:
  7.2 144.8 %copy-start = (bf16[1024,1024]{1,0:T(8,128)(2,1)S(1)}, bf16[1024,1024]{1,0:T(8,128)(2,1)}, u32[]{:S(2)}) copy-start(bf16[1024,1024]{1,0:T(8,128)(2,1)} %param.10) | copy-start | bytes 6291460
  7.2 144.3 %copy-start.4 = (bf16[128,1024]{1,0:T(8,128)(2,1)S(1)}, bf16[128,1024]{1,0:T(8,128)(2,1)}, u32[]{:S(2)}) copy-start(bf16[128,1024]{1,0:T(8,128)(2,1)} %param.9) | copy-start | bytes 786436
  9.5 148.3 %all-to-all-start.4 = ((f32[1,2,64,2,128]{4,1,3,0,2:T(2,128)}), f32[1,2,64,2,128]{4,1,3,0,2:T(2,128)}, u32[]{:S(2)}, u32[]{:S(2)}) async-start(f32[1,2,64,2,128]{4,1,3,0,2:T(2,128)} %copy.40), calls=%async_computation.4 | async-start | bytes 262144 | tf_op jit(solution)/shard_map/all_to_all | solution.py:98
  151.9 2.9 copy-start.6
  151.9 2.9 copy-start.14
  152.0 3.3 copy-start.11
  157.8 20.7 %all-to-all-start = ((f32[1,2,64,2,128]{4,1,3,0,2:T(2,128)}), f32[1,2,64,2,128]{4,1,3,0,2:T(2,128)}, u32[]{:S(2)}, u32[]{:S(2)}) async-start(f32[1,2,64,2,128]{4,1,3,0,2:T(2,128)} %copy.29), calls=%async_computation | async-start | bytes 262144 | tf_op jit(solution)/shard_map/all_to_all | solution.py:98
  178.5 16.4 %all-to-all-start.5 = ((f32[1,128,1,2,128]{4,3,0,2,1:T(2,128)}), f32[1,128,1,2,128]{4,3,0,2,1:T(2,128)}, u32[]{:S(2)}, u32[]{:S(2)}) async-start(f32[1,128,1,2,128]{4,3,0,2,1:T(2,128)} %copy.42), calls=%async_computation.5 | async-start | bytes 262144 | tf_op jit(solution)/shard_map/all_to_all | solution.py:104
  194.9 16.5 %all-to-all-start.1 = ((f32[1,128,1,2,128]{4,3,0,2,1:T(2,128)}), f32[1,128,1,2,128]{4,3,0,2,1:T(2,128)}, u32[]{:S(2)}, u32[]{:S(2)}) async-start(f32[1,128,1,2,128]{4,3,0,2,1:T(2,128)} %copy.32), calls=%async_computation.1 | async-start | bytes 262144 | tf_op jit(solution)/shard_map/all_to_all | solution.py:104
  214.5 3.5 copy-start.8
  214.5 2.6 copy-start.15
  214.5 2.6 copy-start.22
  218.0 3.2 copy-start.13
  222.3 15.2 %all-to-all-start.6 = ((f32[1,2,64,2,128]{4,1,3,0,2:T(2,128)}), f32[1,2,64,2,128]{4,1,3,0,2:T(2,128)}, u32[]{:S(2)}, u32[]{:S(2)}) async-start(f32[1,2,64,2,128]{4,1,3,0,2:T(2,128)} %copy.45), calls=%async_computation.6 | async-start | bytes 262144 | tf_op jit(solution)/shard_map/all_to_all | solution.py:98
  232.9 27.5 %copy-start.16 = (bf16[1024,128]{1,0:T(8,128)(2,1)S(1)}, bf16[1024,128]{1,0:T(8,128)(2,1)}, u32[]{:S(2)}) copy-start(bf16[1024,128]{1,0:T(8,128)(2,1)} %param.11) | copy-start | bytes 786436
  243.0 16.2 %all-to-all-start.7 = ((f32[1,128,1,2,128]{4,3,0,2,1:T(2,128)}), f32[1,128,1,2,128]{4,3,0,2,1:T(2,128)}, u32[]{:S(2)}, u32[]{:S(2)}) async-start(f32[1,128,1,2,128]{4,3,0,2,1:T(2,128)} %copy.47), calls=%async_computation.7 | async-start | bytes 262144 | tf_op jit(solution)/shard_map/all_to_all | solution.py:104
  249.4 302.3 %all-reduce.3.cloned.1.call-start = ((), (), s32[]{:S(2)}) async-start(), calls=%async_computation.8 | async-start | bytes 10485760 | tf_op jit(solution)/shard_map/psum | solution.py:138
  260.5 3.5 copy-start.5
  265.3 4.6 copy-start.3
  265.3 4.6 copy-start.10
  278.1 2.6 copy-start.12
  279.3 15.6 %copy-start.18 = (f32[64,1,1,1,128]{4,1,3,2,0:T(1,128)S(1)}, f32[64,1,1,1,128]{4,1,3,2,0:T(1,128)}, u32[]{:S(2)}) copy-start(f32[64,1,1,1,128]{4,1,3,2,0:T(1,128)} %fusion.56) | copy-start | bytes 98308
  279.3 15.9 %copy-start.17 = (f32[64,1,128]{2,1,0:T(1,128)S(1)}, f32[64,1,128]{2,1,0:T(1,128)}, u32[]{:S(2)}) copy-start(f32[64,1,128]{2,1,0:T(1,128)} %pad_maximum_fusion.1) | copy-start | bytes 98308
  553.6 4.8 copy-start.21
  (8 other events, 9.7 us)
Sparse Core Ops, SparseCore 0:
  278.2 273.3 all-reduce.2
where the time goes:
time: 569 us; the launch traced here: 566 us
  waiting for transfers between devices  269 us (47%)
  local copies, waits for them, and re-layouts  62.4 us (11%)
  matrix products  54.2 us (10%)
  starting transfers between devices  50.1 us (9%)
  loops' own time  48.4 us (9%)
  other arithmetic  39.2 us (7%)
  blocking collectives  27.9 us (5%)
  between operations  15.1 us (3%)
    psum x1, waiting for transfers between devices, body(): lax.psum((total_first, total_middle, total_last), ('lat', 'dp'))  241 us
    another operation x1, loops' own time, legendre(): lax.scan(advance, initial, jnp.arange(1, wave_count).astype(jnp.float32))  48.4 us
    dynamic_slice x63, local copies, waits for them, and re-layouts, legendre(): lax.scan(advance, initial, jnp.arange(1, wave_count).astype(jnp.float32))  40.7 us
    dynamic_update_slice x63, other arithmetic, legendre(): lax.scan(advance, initial, jnp.arange(1, wave_count).astype(jnp.float32))  35.8 us
    all_to_all x3, starting transfers between devices, spectral(): lax.all_to_all(wave_grid, 'lat', split_axis=2, concat_axis=1, tiled=True)  30.2 us
    all_to_all x3, starting transfers between devices, spectral(): lax.all_to_all(back_grid, 'lat', split_axis=1, concat_axis=2, tiled=True)  19.7 us
    all_to_all x3, waiting for transfers between devices, spectral(): lax.all_to_all(back_grid, 'lat', split_axis=1, concat_axis=2, tiled=True)  19.1 us
    all_to_all x1, blocking collectives, spectral(): lax.all_to_all(back_grid, 'lat', split_axis=1, concat_axis=2, tiled=True)  14.1 us
  transfers between devices with their start and end apart: 7, of which 6 were waited for; matrix products, arithmetic and copies ran while one was open for 19% of the time, Pallas kernels for 0%

commit v1 on v0

v1 whole, which is shorter than its diff:
```python
import functools
import math

import jax
import jax.numpy as jnp
import numpy as np
from jax import lax
from jax.experimental import pallas as pl
from jax.experimental.pallas import tpu as pltpu
from jax.sharding import PartitionSpec as P

MW = 64
NLAT = 128
NLON = 256
FEAT = 128
HID = 1024
ROWS = 512
BANDS = 64
BLK = 1280
BF = jnp.bfloat16
F32 = jnp.float32
MESH = pl.DeviceIdType.MESH


def split_terms(table):
    high = table.astype(np.float32).astype(np.dtype(BF))
    low = (table - high.astype(np.float64)).astype(np.float32).astype(np.dtype(BF))
    return np.concatenate([high, high, low], axis=1)


@functools.lru_cache(maxsize=None)
def constant_tables():
    lon = np.arange(NLON)
    wave = np.arange(MW)
    angle = 2.0 * math.pi * ((wave[:, None] * lon[None, :]) % NLON) / NLON
    base = np.concatenate([np.cos(angle), -np.sin(angle)], axis=0)
    factor = np.where(wave == 0, 1.0, 2.0)
    analysis = base / NLON
    synthesis = base * np.concatenate([factor, factor])[:, None]
    to_waves = np.stack([split_terms(analysis), split_terms(synthesis)])
    to_grid = np.stack([split_terms(synthesis.T), split_terms(analysis.T)])

    latitude = (np.arange(NLAT) + 0.5) * (math.pi / NLAT) - 0.5 * math.pi
    mu, cosine = np.sin(latitude), np.cos(latitude)
    quad = cosine * (math.pi / NLAT)
    table = np.zeros((MW, MW + 8, NLAT))
    for m in range(MW):
        steps = np.arange(1, m + 1)
        increments = 0.5 * np.log((2.0 * steps + 1.0) / (2.0 * steps))
        current = np.exp(0.5 * math.log(0.5) + increments.sum() + m * np.log(cosine))
        previous, ratio_prev = np.zeros(NLAT), 1.0
        table[m, 0] = current
        for k in range(1, MW - m):
            n = float(m + k)
            ratio = math.sqrt((4.0 * n * n - 1.0) / (n * n - m * m))
            previous, current = current, ratio * (mu * current - previous / ratio_prev)
            ratio_prev = ratio
            table[m, k] = current
    table = np.concatenate([table[:, :, 0::2], table[:, :, 1::2]], axis=2)
    table[:, MW, :] = quad[0::2][:, None]
    table[:, MW + 1, :] = quad[1::2][:, None]
    return to_waves, to_grid, table.astype(np.float32)


def times(table, value):
    high = value.astype(BF)
    low = (value - high.astype(F32)).astype(BF)
    return jnp.dot(table, jnp.concatenate([high, low, high], axis=0), preferred_element_type=F32)


def terms(table):
    high = table.astype(BF)
    low = (table - high.astype(F32)).astype(BF)
    return jnp.concatenate([high, high, low], axis=1)


def nt(a, b):
    return lax.dot_general(a, b, (((1,), (1,)), ((), ())), preferred_element_type=F32)


def tn(a, b):
    return lax.dot_general(a, b, (((0,), (0,)), ((), ())), preferred_element_type=F32)


def spread(send, waves, kind):
    for lat in range(2):
        for part in range(2):
            send[pl.ds(kind * 4 + lat * 2 + part, BANDS, stride=8), :] = waves[
                part * MW : (part + 1) * MW, lat * FEAT : (lat + 1) * FEAT
            ]


def gather_parts(recv, kind):
    return jnp.concatenate(
        [
            jnp.concatenate(
                [recv[pl.ds(kind * 4 + lat * 2 + part, BANDS, stride=8), :] for lat in range(2)],
                axis=1,
            )
            for part in range(2)
        ],
        axis=0,
    )


def kernel(
    state, cot, w1, w2, w3, tab, tf, ti,
    final, total,
    grads, field, x0, x1, gt, ha0, hb0, da0, db0, ha1, hb1, da1, db1, ga, gb,
    send, recv, core_buf, half_buf, z_buf,
    a2a_send, a2a_recv, core_send, core_recv, rs_send, rs_recv, z_send, z_recv,
):
    me = lax.axis_index("lat")
    dp = lax.axis_index("dp")
    xh, core = dp // 2, lax.rem(dp, 2)
    xl, zy = me // 32, lax.rem(me, 32)
    z, y = zy // 4, lax.rem(zy, 4)
    yh, yl = y // 2, lax.rem(y, 2)
    mate = {"lat": me, "dp": xh * 2 + 1 - core}
    partner = {
        "xa": {"lat": (1 - xl) * 32 + zy, "dp": dp},
        "xb": {"lat": (1 - xl) * 32 + zy, "dp": (1 - xh) * 2 + core},
        "ya": {"lat": xl * 32 + z * 4 + yh * 2 + 1 - yl, "dp": dp},
        "yb": {"lat": xl * 32 + z * 4 + 3 - y, "dp": dp},
    }
    bit = {"xa": lax.rem(xl + xh, 2), "xb": xh, "ya": lax.rem(yl + yh, 2), "yb": yh}

    barrier = pltpu.get_barrier_semaphore()

    def greet(j, carry):
        pl.semaphore_signal(
            barrier, inc=1, device_id={"lat": lax.rem(me + j, BANDS), "dp": dp}, device_id_type=MESH
        )
        return carry

    lax.fori_loop(1, BANDS, greet, 0)
    for other in (mate, partner["xb"]):
        pl.semaphore_signal(barrier, inc=1, device_id=other, device_id_type=MESH)

    def forward(lat, x, source, ha, hb, da, db):
        rows = pl.ds(pl.multiple_of(lat * NLON, NLON), NLON)
        mine = x[rows, :]
        for layer in range(2):
            weight, act, slope = ((w1, ha, da), (w2, hb, db))[layer]
            rows_in = mine if layer == 0 else ha[rows, :]
            for n in range(4):
                cols = slice(n * 256, (n + 1) * 256)
                pre = jnp.dot(rows_in, weight[:, cols], preferred_element_type=F32)
                gate = jax.nn.sigmoid(pre)
                out = pre * gate
                act[rows, cols] = out.astype(BF)
                slope[rows, cols] = gate * (1.0 + pre * (1.0 - gate))
        tend = jnp.dot(hb[rows, :], w3[...], preferred_element_type=F32)
        field[rows, :] = source[rows, :] + 0.5 * tend

    def backward(lat, da, db, pulled, want_rows):
        rows = pl.ds(pl.multiple_of(lat * NLON, NLON), NLON)
        scaled = gt[rows, :]
        for n in range(4):
            cols = slice(n * 256, (n + 1) * 256)
            gb[rows, cols] = (nt(scaled, w3[cols, :]) * db[rows, cols]).astype(BF)
        grad_b = gb[rows, :]
        for n in range(4):
            cols = slice(n * 256, (n + 1) * 256)
            ga[rows, cols] = (nt(grad_b, w2[cols, :]) * da[rows, cols]).astype(BF)
        if want_rows:
            pulled[rows, :] = pulled[rows, :] + nt(ga[rows, :], w1[...])

    def weight_grads(x, ha, hb, add):
        def put(start, value):
            for half in range(2):
                block = value[:, half * 128 : (half + 1) * 128]
                rows = pl.ds(pl.multiple_of(start + half * BLK, 128), block.shape[0])
                grads[rows, :] = block + grads[rows, :] if add else block

        def middle(i, carry):
            left = ha[:, pl.ds(pl.multiple_of(i * 256, 256), 256)]
            for n in range(4):
                put(2 * n * BLK + i * 256, tn(left, gb[:, n * 256 : (n + 1) * 256]))
            return carry

        lax.fori_loop(0, 4, middle, 0)
        for n in range(4):
            cols = slice(n * 256, (n + 1) * 256)
            put(2 * n * BLK + 1024, tn(x[...], ga[:, cols]))
            put(2 * n * BLK + 1152, tn(gt[...], hb[:, cols]))

    def lanes(ref):
        return jnp.concatenate([ref[0:NLON, :], ref[NLON : 2 * NLON, :]], axis=1)

    quad = jnp.concatenate([tab[MW : MW + 1, :], tab[MW + 1 : MW + 2, :]], axis=1)

    def to_waves(ref, kind, out):
        waves = times(tf[kind], lanes(ref))
        spread(out, waves * quad if kind == 0 else waves, kind)

    def to_grid(source, kind):
        value = times(ti[kind], gather_parts(source, kind))
        return value if kind == 0 else value * quad

    def exchange(index):
        out, into = send.at[index], recv.at[index]
        mine = pl.ds(pl.multiple_of(me * 8, 8), 8)

        def start(j, carry):
            target = lax.rem(me + 18 + j + j // 46, BANDS)
            pltpu.make_async_remote_copy(
                src_ref=out.at[pl.ds(pl.multiple_of(target * 8, 8), 8), :],
                dst_ref=into.at[mine, :],
                send_sem=a2a_send.at[index],
                recv_sem=a2a_recv.at[index],
                device_id={"lat": target, "dp": dp},
                device_id_type=MESH,
            ).start()
            return carry

        lax.fori_loop(0, BANDS - 1, start, 0)
        recv[index, mine, :] = send[index, mine, :]

    def arrive(index):
        most = pl.ds(0, 8 * (BANDS - 1))
        pltpu.make_async_copy(recv.at[index, most, :], recv.at[index, most, :], a2a_recv.at[index]).wait()
        pltpu.make_async_copy(send.at[index, most, :], send.at[index, most, :], a2a_send.at[index]).wait()

    def legendre(source, target):
        degree = me + lax.broadcasted_iota(jnp.int32, (MW, NLAT), 0)
        size = (degree * (degree + 1)).astype(F32)
        damping = jnp.where(degree <= MW - 1, 1.0 / (1.0 + size / (MW * (MW - 1.0))), 0.0)
        poly = tab[0:MW, :]
        columns = [(kind, part) for kind in range(2) for part in range(2)]
        value = jnp.concatenate(
            [
                jnp.concatenate(
                    [source[pl.ds(kind * 4 + lat * 2 + part, BANDS, stride=8), :] for lat in range(2)],
                    axis=0,
                )
                for kind, part in columns
            ],
            axis=1,
        )
        coeffs = times(terms(poly * damping), value)
        back = times(terms(poly.T), coeffs)
        for i, (kind, part) in enumerate(columns):
            for lat in range(2):
                target[pl.ds(kind * 4 + lat * 2 + part, BANDS, stride=8), :] = back[
                    lat * BANDS : (lat + 1) * BANDS, i * FEAT : (i + 1) * FEAT
                ]

    def both(step):
        def run(lat, carry):
            step(lat)
            return carry

        lax.fori_loop(0, 2, run, 0)

    to_waves(cot, 1, send.at[0])
    x0[...] = state[...].astype(BF)
    both(lambda lat: forward(lat, x0, state, ha0, hb0, da0, db0))
    to_waves(field, 0, send.at[0])
    pl.semaphore_wait(barrier, BANDS + 1)
    exchange(0)
    arrive(0)
    legendre(recv.at[0], send.at[1])
    exchange(1)
    arrive(1)

    value = to_grid(recv.at[1], 0)
    pulled = to_grid(recv.at[1], 1)
    for lat in range(2):
        rows, cols = slice(lat * NLON, (lat + 1) * NLON), slice(lat * FEAT, (lat + 1) * FEAT)
        field[rows, :] = value[:, cols]
        x1[rows, :] = value[:, cols].astype(BF)
        final[rows, :] = pulled[:, cols]
        gt[rows, :] = (0.5 * pulled[:, cols]).astype(BF)
    both(lambda lat: forward(lat, x1, field, ha1, hb1, da1, db1))
    to_waves(field, 0, send.at[2])
    both(lambda lat: backward(lat, da1, db1, final, True))
    to_waves(final, 1, send.at[2])
    exchange(2)
    weight_grads(x1, ha1, hb1, False)
    arrive(2)
    legendre(recv.at[2], send.at[3])
    exchange(3)
    arrive(3)

    pulled = to_grid(recv.at[3], 1)
    for lat in range(2):
        rows, cols = slice(lat * NLON, (lat + 1) * NLON), slice(lat * FEAT, (lat + 1) * FEAT)
        gt[rows, :] = (0.5 * pulled[:, cols]).astype(BF)
    both(lambda lat: backward(lat, da0, db0, None, False))
    weight_grads(x0, ha0, hb0, True)
    value = to_grid(recv.at[3], 0)
    for lat in range(2):
        rows, cols = slice(lat * NLON, (lat + 1) * NLON), slice(lat * FEAT, (lat + 1) * FEAT)
        final[rows, :] = value[:, cols]

    def tiles(ref, start, count):
        return ref.at[pl.ds(pl.multiple_of(start * 8, 8), count * 8), :]

    def add(start, source, source_start, count):
        def one(i, carry):
            for j in range(5):
                into = pl.ds(pl.multiple_of((start + i * 5 + j) * 8, 8), 8)
                rows = pl.ds(pl.multiple_of((source_start + i * 5 + j) * 8, 8), 8)
                grads[into, :] = grads[into, :] + source[rows, :]
            return carry

        lax.fori_loop(0, count // 5, one, 0)

    def copy(source, target, send_sem, recv_sem, device):
        return pltpu.make_async_remote_copy(
            src_ref=source, dst_ref=target, send_sem=send_sem, recv_sem=recv_sem,
            device_id=device, device_id_type=MESH,
        )

    order = (
        ("xa", "xb", "ya", "yb"),
        ("xb", "xa", "yb", "ya"),
        ("ya", "yb", "xa", "xb"),
        ("yb", "ya", "xb", "xa"),
    )
    size = 160
    starts = []
    for s in range(4):
        c = copy(
            tiles(grads, (1 - core) * 640 + s * size, size), tiles(core_buf, s * size, size),
            core_send.at[s], core_recv.at[s], mate,
        )
        c.start()
        starts.append(c)
    offset = [core * 640 + s * size for s in range(4)]
    for s in range(4):
        starts[s].wait()
        add(offset[s], core_buf, s * size, size)
    kept = [[o] for o in offset]
    place = 0
    running = {}
    for step in range(5):
        count = size >> (step + 1)
        for s in range(4):
            if step > 0:
                c, keep, base = running[s]
                c.wait()
                add(keep, half_buf, base, count * 2)
                kept[s].append(keep)
            if step < 4:
                name = order[s][step]
                now = kept[s][step]
                keep = now + bit[name] * count
                gone = now + (1 - bit[name]) * count
                c = copy(
                    tiles(grads, gone, count), tiles(half_buf, place, count),
                    rs_send.at[step * 4 + s], rs_recv.at[step * 4 + s], partner[name],
                )
                c.start()
                running[s] = (c, keep, place)
                place += count

    def chunk(index):
        which = index // 2
        start = jnp.where(
            which == 0,
            kept[0][4],
            jnp.where(which == 1, kept[1][4], jnp.where(which == 2, kept[2][4], kept[3][4])),
        )
        return start + 5 * lax.rem(index, 2)

    own = chunk(z)
    zs = []
    for i in range(1, 8):
        other = lax.rem(z + i, 8)
        c = copy(
            tiles(grads, chunk(other), 5), tiles(z_buf, 5 * (i - 1), 5),
            z_send.at[i - 1], z_recv.at[i - 1], {"lat": xl * 32 + other * 4 + y, "dp": dp},
        )
        c.start()
        zs.append(c)
    for c in zs:
        c.wait()
    for j in range(5):
        rows = pl.ds(pl.multiple_of((own + j) * 8, 8), 8)
        value = grads[rows, :]
        for i in range(7):
            value = value + z_buf[(5 * i + j) * 8 : (5 * i + j + 1) * 8, :]
        total[rows, :] = value

    zs = []
    for i in range(1, 8):
        other = lax.rem(z + i, 8)
        c = copy(
            tiles(total, own, 5), tiles(total, own, 5),
            z_send.at[6 + i], z_recv.at[6 + i], {"lat": xl * 32 + other * 4 + y, "dp": dp},
        )
        c.start()
        zs.append(c)
    for c in zs:
        c.wait()
    running = {}
    for step in (3, 2, 1, 0, -1):
        for s in range(4):
            if step < 3:
                running[s].wait()
            if step >= 0:
                count = size >> (step + 1)
                held = tiles(total, kept[s][step + 1], count)
                sem = 16 + step * 4 + s
                c = copy(held, held, rs_send.at[sem], rs_recv.at[sem], partner[order[s][step]])
            else:
                held = tiles(total, offset[s], size)
                c = copy(held, held, core_send.at[4 + s], core_recv.at[4 + s], mate)
            c.start()
            running[s] = c
    for s in range(4):
        running[s].wait()


def body(state, cotangent, w_first, w_middle, w_last):
    to_waves, to_grid, table = constant_tables()
    tab = lax.dynamic_index_in_dim(jnp.asarray(table), lax.axis_index("lat"), 0, keepdims=False)
    vmem = pl.BlockSpec(memory_space=pltpu.VMEM)
    act = pltpu.VMEM((ROWS, HID), BF)
    slope = pltpu.VMEM((ROWS, HID), F32)
    thin = pltpu.VMEM((ROWS, FEAT), BF)
    dma = pltpu.SemaphoreType.DMA
    final, grads = pl.pallas_call(
        kernel,
        out_shape=(
            jax.ShapeDtypeStruct((ROWS, FEAT), F32),
            jax.ShapeDtypeStruct((8 * BLK, 128), F32),
        ),
        in_specs=[vmem] * 8,
        out_specs=(vmem, vmem),
        scratch_shapes=[
            pltpu.VMEM((8 * BLK, 128), F32), pltpu.VMEM((ROWS, FEAT), F32), thin, thin, thin,
            act, act, slope, slope, act, act, slope, slope, act, act,
            pltpu.VMEM((4, 8 * BANDS, FEAT), F32), pltpu.VMEM((4, 8 * BANDS, FEAT), F32),
            pltpu.VMEM((640 * 8, 128), F32), pltpu.VMEM((600 * 8, 128), F32),
            pltpu.VMEM((35 * 8, 128), F32),
            dma((4,)), dma((4,)), dma((8,)), dma((8,)), dma((32,)), dma((32,)), dma((14,)), dma((14,)),
        ],
        compiler_params=pltpu.CompilerParams(
            collective_id=0, has_side_effects=True, vmem_limit_bytes=60 * 1024 * 1024
        ),
        name="spectral_steps",
    )(
        state.reshape(ROWS, FEAT), cotangent.reshape(ROWS, FEAT), w_first, w_middle, w_last,
        tab, jnp.asarray(to_waves), jnp.asarray(to_grid),
    )
    blocks = grads.reshape(8, BLK, 128)

    def columns(piece):
        return piece.transpose(1, 0, 2).reshape(piece.shape[1], HID)

    return (
        final.reshape(state.shape),
        columns(blocks[:, 1024:1152]),
        columns(blocks[:, :1024]),
        columns(blocks[:, 1152:]).T,
    )


def solution(mesh):
    in_specs = (P("dp", "lat", None, None), P("dp", "lat", None, None), P(), P(), P())
    out_specs = (P("dp", "lat", None, None), P(), P(), P())
    return jax.shard_map(body, mesh=mesh, in_specs=in_specs, out_specs=out_specs, check_vma=False)
```

time: 569 us -> 142 us (0.25)
  waiting for transfers between devices: 269 us -> 0 us
  Pallas kernels: 0 us -> 131 us
  matrix products: 54.2 us -> 0 us
  local copies, waits for them, and re-layouts: 62.4 us -> 10 us
  starting transfers between devices: 50.1 us -> 0 us
  loops' own time: 48.4 us -> 0 us
  other arithmetic: 39.2 us -> 0 us
  blocking collectives: 27.9 us -> 0 us
  between operations: 15.1 us -> 0.66 us
    psum x1 -> x0, waiting for transfers between devices: 241 us -> none  [body(): lax.psum((total_first, total_middle, total_last), ('lat', 'dp'))]
    pallas_call x0 -> x1, Pallas kernels: none -> 131 us  [body(): pl.pallas_call(kernel, out_shape=(jax.ShapeDtypeStruct((ROWS, FEAT), F32)...]
    dot_general x32 -> x0, matrix products: 54.2 us -> none  [the longest x2 11.1 us: body(): jnp.dot(hidden_first.T, middle_grad, preferred_element_type=jnp.float32)]
    all_to_all x6 -> x0, starting transfers between devices: 49.8 us -> none  [the longest x3 30.2 us: spectral(): lax.all_to_all(wave_grid, 'lat', split_axis=2, concat_axis=1, tiled=True)]
    another operation x1 -> x0, loops' own time: 48.4 us -> none  [legendre(): lax.scan(advance, initial, jnp.arange(1, wave_count).astype(jnp.float32))]
    dynamic_slice x63 -> x0, local copies, waits for them, and re-layouts: 40.7 us -> none  [legendre(): lax.scan(advance, initial, jnp.arange(1, wave_count).astype(jnp.float32))]
    dynamic_update_slice x63 -> x0, other arithmetic: 35.8 us -> none  [legendre(): lax.scan(advance, initial, jnp.arange(1, wave_count).astype(jnp.float32))]
    all_to_all x6 -> x0, waiting for transfers between devices: 28 us -> none  [the longest x3 19.1 us: spectral(): lax.all_to_all(back_grid, 'lat', split_axis=1, concat_axis=2, tiled=True)]
  transfers between devices with their start and end apart: 7 -> 0, of which waited for: 6 -> 0; matrix products, arithmetic and copies ran while one was open for 19% -> 0% of each run, Pallas kernels for 0% -> 0%
where the time goes in v1:
time: 142 us
  Pallas kernels  131 us (92%)
  local copies, waits for them, and re-layouts  10 us (7%)
    pallas_call x1, Pallas kernels, body(): pl.pallas_call(kernel, out_shape=(jax.ShapeDtypeStruct((ROWS, FEAT), F32)...  131 us
    reshape x2, local copies, waits for them, and re-layouts, columns(): return piece.transpose(1, 0, 2).reshape(piece.shape[1], HID)  5.68 us

profile of v1, /device:TPU:1, one launch (start us, length us, event | category | flops | bytes accessed | tf_op | source)
XLA Modules:
  0.0 141.7 jit_solution(16724331094032937363)
XLA Ops:
  0.6 1.4 dynamic-slice_bitcast_fusion.tab
  2.0 131.0 %spectral_steps.1 = (f32[512,128]{1,0:T(8,128)}, f32[10240,128]{1,0:T(8,128)}) custom-call(f32[512,128]{1,0:T(8,128)} %bitcast.27, f32[512,128]{1,0:T(8,128)} %bitcast.28, bf16[128,1024]{1,0:T(8,128)(2,1)} %w1.1, bf16[1024,1024]{1,0:T(8,128)(2,1)} %w2.1, bf16[1024,128]{1,0:T(8,128)(2,1)} %w3.1, f32[72,128]{1,0:T(8,128)} %dynamic-slice_bitcast_fusion.tab, ...), custom_call_target="tpu_custom_call" | custom-call | tf_op jit(solution)/shard_map/spectral_steps/pallas_call | solution.py:425
  133.0 1.3 slice_bitcast_fusion.1
  134.3 0.0 copy-start
  134.3 4.8 %copy_bitcast_fusion = f32[1024,1024]{1,0:T(8,128)} fusion(f32[8,1280,128]{2,1,0:T(8,128)} %bitcast.24), kind=kLoop, calls=%fused_computation | loop fusion | bytes 8388608 | tf_op jit(solution)/shard_map/reshape | solution.py:452
  139.1 1.0 copy.14
  140.1 0.8 copy.19
  141.0 0.0 copy-done
  141.0 0.7 copy.21
Async XLA Ops:
  134.3 6.7 %copy-start = (f32[512,128]{1,0:T(8,128)S(1)}, f32[512,128]{1,0:T(8,128)}, u32[]{:S(2)}) copy-start(f32[512,128]{1,0:T(8,128)} %get-tuple-element.6) | copy-start | bytes 786436

commit v2 on v1

--- a/solution.py
+++ b/solution.py
@@ -43,7 +43,7 @@
     latitude = (np.arange(NLAT) + 0.5) * (math.pi / NLAT) - 0.5 * math.pi
     mu, cosine = np.sin(latitude), np.cos(latitude)
     quad = cosine * (math.pi / NLAT)
-    table = np.zeros((MW, MW + 8, NLAT))
+    table = np.zeros((MW, MW, NLAT))
     for m in range(MW):
         steps = np.arange(1, m + 1)
         increments = 0.5 * np.log((2.0 * steps + 1.0) / (2.0 * steps))
@@ -57,9 +57,8 @@
             ratio_prev = ratio
             table[m, k] = current
     table = np.concatenate([table[:, :, 0::2], table[:, :, 1::2]], axis=2)
-    table[:, MW, :] = quad[0::2][:, None]
-    table[:, MW + 1, :] = quad[1::2][:, None]
-    return to_waves, to_grid, table.astype(np.float32)
+    packed = [table[m, : MW - 8 * (m // 8)] for m in range(MW)] + [np.zeros((MW - 8, NLAT))]
+    return to_waves, to_grid, np.concatenate(packed).astype(np.float32), quad.astype(np.float32)
 
 
 def times(table, value):
@@ -104,11 +103,12 @@
 
 
 def kernel(
+    state_in, cot_in, w1_in, w2_in, w3_in, tab_in, tf_in, ti_in, quad_in,
+    final, total,
     state, cot, w1, w2, w3, tab, tf, ti,
-    final, total,
     grads, field, x0, x1, gt, ha0, hb0, da0, db0, ha1, hb1, da1, db1, ga, gb,
     send, recv, core_buf, half_buf, z_buf,
-    a2a_send, a2a_recv, core_send, core_recv, rs_send, rs_recv, z_send, z_recv,
+    loads, a2a_send, a2a_recv, core_send, core_recv, rs_send, rs_recv, z_send, z_recv,
 ):
     me = lax.axis_index("lat")
     dp = lax.axis_index("dp")
@@ -125,6 +125,19 @@
     }
     bit = {"xa": lax.rem(xl + xh, 2), "xb": xh, "ya": lax.rem(yl + yh, 2), "yb": yh}
 
+    group = me // 8
+    first_row = 64 * (8 * group - group * (group - 1) // 2) + lax.rem(me, 8) * (8 - group) * 8
+    wanted = {
+        "cot": (cot_in, cot), "tf": (tf_in, tf), "state": (state_in, state), "w1": (w1_in, w1),
+        "w2": (w2_in, w2), "w3": (w3_in, w3), "ti": (ti_in, ti),
+        "tab": (tab_in.at[pl.ds(pl.multiple_of(first_row, 8), MW), :], tab),
+    }
+    loading = {
+        name: pltpu.make_async_copy(a, b, loads.at[i]) for i, (name, (a, b)) in enumerate(wanted.items())
+    }
+    for c in loading.values():
+        c.start()
+
     barrier = pltpu.get_barrier_semaphore()
 
     def greet(j, carry):
@@ -167,9 +180,10 @@
             pulled[rows, :] = pulled[rows, :] + nt(ga[rows, :], w1[...])
 
     def weight_grads(x, ha, hb, add):
-        def put(start, value):
+        def put(start, value, flip=False):
             for half in range(2):
                 block = value[:, half * 128 : (half + 1) * 128]
+                block = block.T if flip else block
                 rows = pl.ds(pl.multiple_of(start + half * BLK, 128), block.shape[0])
                 grads[rows, :] = block + grads[rows, :] if add else block
 
@@ -183,12 +197,12 @@
         for n in range(4):
             cols = slice(n * 256, (n + 1) * 256)
             put(2 * n * BLK + 1024, tn(x[...], ga[:, cols]))
-            put(2 * n * BLK + 1152, tn(gt[...], hb[:, cols]))
+            put(2 * n * BLK + 1152, tn(gt[...], hb[:, cols]), True)
 
     def lanes(ref):
         return jnp.concatenate([ref[0:NLON, :], ref[NLON : 2 * NLON, :]], axis=1)
 
-    quad = jnp.concatenate([tab[MW : MW + 1, :], tab[MW + 1 : MW + 2, :]], axis=1)
+    quad = jnp.concatenate([jnp.full((1, FEAT), quad_in[2 * me + lat], F32) for lat in range(2)], axis=1)
 
     def to_waves(ref, kind, out):
         waves = times(tf[kind], lanes(ref))
@@ -198,53 +212,59 @@
         value = times(ti[kind], gather_parts(source, kind))
         return value if kind == 0 else value * quad
 
-    def exchange(index):
-        out, into = send.at[index], recv.at[index]
-        mine = pl.ds(pl.multiple_of(me * 8, 8), 8)
-
+    def piece(ref, index, device, kind):
+        return ref.at[index, pl.ds(pl.multiple_of(device * 8, 8), 8), :].at[pl.ds(4 * kind, 4), :]
+
+    def exchange(index, kind):
         def start(j, carry):
             target = lax.rem(me + 18 + j + j // 46, BANDS)
             pltpu.make_async_remote_copy(
-                src_ref=out.at[pl.ds(pl.multiple_of(target * 8, 8), 8), :],
-                dst_ref=into.at[mine, :],
-                send_sem=a2a_send.at[index],
-                recv_sem=a2a_recv.at[index],
+                src_ref=piece(send, index, target, kind),
+                dst_ref=piece(recv, index, me, kind),
+                send_sem=a2a_send.at[2 * index + kind],
+                recv_sem=a2a_recv.at[2 * index + kind],
                 device_id={"lat": target, "dp": dp},
                 device_id_type=MESH,
             ).start()
             return carry
 
         lax.fori_loop(0, BANDS - 1, start, 0)
+        mine = pl.ds(pl.multiple_of(me * 8, 8) + 4 * kind, 4)
         recv[index, mine, :] = send[index, mine, :]
 
-    def arrive(index):
-        most = pl.ds(0, 8 * (BANDS - 1))
-        pltpu.make_async_copy(recv.at[index, most, :], recv.at[index, most, :], a2a_recv.at[index]).wait()
-        pltpu.make_async_copy(send.at[index, most, :], send.at[index, most, :], a2a_send.at[index]).wait()
-
-    def legendre(source, target):
+    def arrive(index, kind):
+        most = pl.ds(0, 4 * (BANDS - 1))
+        for ref, sem in ((recv, a2a_recv), (send, a2a_send)):
+            half = ref.at[index, most, :]
+            pltpu.make_async_copy(half, half, sem.at[2 * index + kind]).wait()
+
+    def legendre(source, target, kind):
         degree = me + lax.broadcasted_iota(jnp.int32, (MW, NLAT), 0)
         size = (degree * (degree + 1)).astype(F32)
         damping = jnp.where(degree <= MW - 1, 1.0 / (1.0 + size / (MW * (MW - 1.0))), 0.0)
-        poly = tab[0:MW, :]
-        columns = [(kind, part) for kind in range(2) for part in range(2)]
+        poly = tab[...]
         value = jnp.concatenate(
             [
                 jnp.concatenate(
                     [source[pl.ds(kind * 4 + lat * 2 + part, BANDS, stride=8), :] for lat in range(2)],
                     axis=0,
                 )
-                for kind, part in columns
+                for part in range(2)
             ],
             axis=1,
         )
         coeffs = times(terms(poly * damping), value)
         back = times(terms(poly.T), coeffs)
-        for i, (kind, part) in enumerate(columns):
+        for part in range(2):
             for lat in range(2):
                 target[pl.ds(kind * 4 + lat * 2 + part, BANDS, stride=8), :] = back[
-                    lat * BANDS : (lat + 1) * BANDS, i * FEAT : (i + 1) * FEAT
+                    lat * BANDS : (lat + 1) * BANDS, part * FEAT : (part + 1) * FEAT
                 ]
+
+    def turn(index, kind):
+        arrive(index, kind)
+        legendre(recv.at[index], send.at[index + 1], kind)
+        exchange(index + 1, kind)
 
     def both(step):
         def run(lat, carry):
@@ -253,46 +273,56 @@
 
         lax.fori_loop(0, 2, run, 0)
 
+    for name in ("cot", "tf"):
+        loading[name].wait()
     to_waves(cot, 1, send.at[0])
+    for name in ("state", "w1", "w2", "w3"):
+        loading[name].wait()
     x0[...] = state[...].astype(BF)
-    both(lambda lat: forward(lat, x0, state, ha0, hb0, da0, db0))
+
+    def opening(lat):
+        forward(lat, x0, state, ha0, hb0, da0, db0)
+
+        @pl.when(lat == 0)
+        def _():
+            pl.semaphore_wait(barrier, BANDS + 1)
+            exchange(0, 1)
+
+    both(opening)
     to_waves(field, 0, send.at[0])
-    pl.semaphore_wait(barrier, BANDS + 1)
-    exchange(0)
-    arrive(0)
-    legendre(recv.at[0], send.at[1])
-    exchange(1)
-    arrive(1)
-
+    exchange(0, 0)
+    for name in ("ti", "tab"):
+        loading[name].wait()
+    turn(0, 1)
+    turn(0, 0)
+
+    halves = [(slice(lat * NLON, (lat + 1) * NLON), slice(lat * FEAT, (lat + 1) * FEAT)) for lat in range(2)]
+    arrive(1, 0)
     value = to_grid(recv.at[1], 0)
-    pulled = to_grid(recv.at[1], 1)
-    for lat in range(2):
-        rows, cols = slice(lat * NLON, (lat + 1) * NLON), slice(lat * FEAT, (lat + 1) * FEAT)
+    for rows, cols in halves:
         field[rows, :] = value[:, cols]
         x1[rows, :] = value[:, cols].astype(BF)
+    both(lambda lat: forward(lat, x1, field, ha1, hb1, da1, db1))
+    to_waves(field, 0, send.at[2])
+    exchange(2, 0)
+    arrive(1, 1)
+    pulled = to_grid(recv.at[1], 1)
+    for rows, cols in halves:
         final[rows, :] = pulled[:, cols]
         gt[rows, :] = (0.5 * pulled[:, cols]).astype(BF)
-    both(lambda lat: forward(lat, x1, field, ha1, hb1, da1, db1))
-    to_waves(field, 0, send.at[2])
     both(lambda lat: backward(lat, da1, db1, final, True))
     to_waves(final, 1, send.at[2])
-    exchange(2)
+    exchange(2, 1)
     weight_grads(x1, ha1, hb1, False)
-    arrive(2)
-    legendre(recv.at[2], send.at[3])
-    exchange(3)
-    arrive(3)
-
+    turn(2, 1)
+    turn(2, 0)
+
+    arrive(3, 1)
     pulled = to_grid(recv.at[3], 1)
-    for lat in range(2):
-        rows, cols = slice(lat * NLON, (lat + 1) * NLON), slice(lat * FEAT, (lat + 1) * FEAT)
+    for rows, cols in halves:
         gt[rows, :] = (0.5 * pulled[:, cols]).astype(BF)
     both(lambda lat: backward(lat, da0, db0, None, False))
     weight_grads(x0, ha0, hb0, True)
-    value = to_grid(recv.at[3], 0)
-    for lat in range(2):
-        rows, cols = slice(lat * NLON, (lat + 1) * NLON), slice(lat * FEAT, (lat + 1) * FEAT)
-        final[rows, :] = value[:, cols]
 
     def tiles(ref, start, count):
         return ref.at[pl.ds(pl.multiple_of(start * 8, 8), count * 8), :]
@@ -319,51 +349,53 @@
         ("ya", "yb", "xa", "xb"),
         ("yb", "ya", "xb", "xa"),
     )
-    size = 160
+    size = 80
+    parts = range(8)
     starts = []
-    for s in range(4):
+    for s in parts:
         c = copy(
             tiles(grads, (1 - core) * 640 + s * size, size), tiles(core_buf, s * size, size),
             core_send.at[s], core_recv.at[s], mate,
         )
         c.start()
         starts.append(c)
-    offset = [core * 640 + s * size for s in range(4)]
-    for s in range(4):
-        starts[s].wait()
-        add(offset[s], core_buf, s * size, size)
+    arrive(3, 0)
+    value = to_grid(recv.at[3], 0)
+    for rows, cols in halves:
+        final[rows, :] = value[:, cols]
+    offset = [core * 640 + s * size for s in parts]
     kept = [[o] for o in offset]
     place = 0
     running = {}
     for step in range(5):
         count = size >> (step + 1)
-        for s in range(4):
-            if step > 0:
+        for s in parts:
+            if step == 0:
+                starts[s].wait()
+                add(offset[s], core_buf, s * size, size)
+            else:
                 c, keep, base = running[s]
                 c.wait()
-                add(keep, half_buf, base, count * 2)
+                add(keep, half_buf, base, size >> step)
                 kept[s].append(keep)
             if step < 4:
-                name = order[s][step]
+                name = order[s % 4][step]
                 now = kept[s][step]
                 keep = now + bit[name] * count
                 gone = now + (1 - bit[name]) * count
                 c = copy(
                     tiles(grads, gone, count), tiles(half_buf, place, count),
-                    rs_send.at[step * 4 + s], rs_recv.at[step * 4 + s], partner[name],
+                    rs_send.at[step * 8 + s], rs_recv.at[step * 8 + s], partner[name],
                 )
                 c.start()
                 running[s] = (c, keep, place)
                 place += count
 
     def chunk(index):
-        which = index // 2
-        start = jnp.where(
-            which == 0,
-            kept[0][4],
-            jnp.where(which == 1, kept[1][4], jnp.where(which == 2, kept[2][4], kept[3][4])),
-        )
-        return start + 5 * lax.rem(index, 2)
+        start = kept[7][4]
+        for s in range(7):
+            start = jnp.where(index == s, kept[s][4], start)
+        return start
 
     own = chunk(z)
     zs = []
@@ -396,67 +428,94 @@
     for c in zs:
         c.wait()
     running = {}
+    last = []
     for step in (3, 2, 1, 0, -1):
-        for s in range(4):
+        for s in parts:
             if step < 3:
                 running[s].wait()
             if step >= 0:
                 count = size >> (step + 1)
                 held = tiles(total, kept[s][step + 1], count)
-                sem = 16 + step * 4 + s
-                c = copy(held, held, rs_send.at[sem], rs_recv.at[sem], partner[order[s][step]])
-            else:
-                held = tiles(total, offset[s], size)
-                c = copy(held, held, core_send.at[4 + s], core_recv.at[4 + s], mate)
-            c.start()
-            running[s] = c
-    for s in range(4):
-        running[s].wait()
+                sem = 32 + step * 8 + s
+                c = copy(held, held, rs_send.at[sem], rs_recv.at[sem], partner[order[s % 4][step]])
+                c.start()
+                running[s] = c
+            if step <= 0:
+                first = kept[s][1] if step == 0 else 2 * kept[s][0] + size // 2 - kept[s][1]
+                held = tiles(total, first, size // 2)
+                sem = 16 + 8 * step + s
+                c = copy(held, held, core_send.at[8 + sem], core_recv.at[8 + sem], mate)
+                c.start()
+                last.append(c)
+    for c in last:
+        c.wait()
+
+
+def write_out(final, total, field, first, middle, last, sems):
+    copies = [(final, field)]
+    for c in range(8):
+        cols = pl.ds(c * 128, 128)
+        copies.append((total.at[pl.ds(c * BLK, 1024), :], middle.at[:, cols]))
+        copies.append((total.at[pl.ds(c * BLK + 1024, 128), :], first.at[:, cols]))
+        copies.append((total.at[pl.ds(c * BLK + 1152, 128), :], last.at[cols, :]))
+    running = [pltpu.make_async_copy(a, b, sems.at[i]) for i, (a, b) in enumerate(copies)]
+    for c in running:
+        c.start()
+    for c in running:
+        c.wait()
 
 
 def body(state, cotangent, w_first, w_middle, w_last):
-    to_waves, to_grid, table = constant_tables()
-    tab = lax.dynamic_index_in_dim(jnp.asarray(table), lax.axis_index("lat"), 0, keepdims=False)
+    to_waves, to_grid, table, quad = constant_tables()
+    hbm = pl.BlockSpec(memory_space=pltpu.HBM)
     vmem = pl.BlockSpec(memory_space=pltpu.VMEM)
     act = pltpu.VMEM((ROWS, HID), BF)
     slope = pltpu.VMEM((ROWS, HID), F32)
     thin = pltpu.VMEM((ROWS, FEAT), BF)
     dma = pltpu.SemaphoreType.DMA
-    final, grads = pl.pallas_call(
+    final, total = pl.pallas_call(
         kernel,
         out_shape=(
-            jax.ShapeDtypeStruct((ROWS, FEAT), F32),
-            jax.ShapeDtypeStruct((8 * BLK, 128), F32),
+            pltpu.VMEM((ROWS, FEAT), F32),
+            pltpu.VMEM((8 * BLK, 128), F32),
         ),
-        in_specs=[vmem] * 8,
+        in_specs=[hbm] * 8 + [pl.BlockSpec(memory_space=pltpu.SMEM)],
         out_specs=(vmem, vmem),
         scratch_shapes=[
+            pltpu.VMEM((ROWS, FEAT), F32), pltpu.VMEM((ROWS, FEAT), F32),
+            pltpu.VMEM((FEAT, HID), BF), pltpu.VMEM((HID, HID), BF), pltpu.VMEM((HID, FEAT), BF),
+            pltpu.VMEM((MW, NLAT), F32), pltpu.VMEM(to_waves.shape, BF), pltpu.VMEM(to_grid.shape, BF),
             pltpu.VMEM((8 * BLK, 128), F32), pltpu.VMEM((ROWS, FEAT), F32), thin, thin, thin,
             act, act, slope, slope, act, act, slope, slope, act, act,
             pltpu.VMEM((4, 8 * BANDS, FEAT), F32), pltpu.VMEM((4, 8 * BANDS, FEAT), F32),
             pltpu.VMEM((640 * 8, 128), F32), pltpu.VMEM((600 * 8, 128), F32),
             pltpu.VMEM((35 * 8, 128), F32),
-            dma((4,)), dma((4,)), dma((8,)), dma((8,)), dma((32,)), dma((32,)), dma((14,)), dma((14,)),
+            dma((8,)), dma((8,)), dma((8,)), dma((32,)), dma((32,)), dma((64,)), dma((64,)), dma((14,)), dma((14,)),
         ],
         compiler_params=pltpu.CompilerParams(
-            collective_id=0, has_side_effects=True, vmem_limit_bytes=60 * 1024 * 1024
+            collective_id=0, has_side_effects=True, vmem_limit_bytes=57 * 1024 * 1024
         ),
         name="spectral_steps",
     )(
         state.reshape(ROWS, FEAT), cotangent.reshape(ROWS, FEAT), w_first, w_middle, w_last,
-        tab, jnp.asarray(to_waves), jnp.asarray(to_grid),
+        jnp.asarray(table), jnp.asarray(to_waves), jnp.asarray(to_grid), jnp.asarray(quad),
     )
-    blocks = grads.reshape(8, BLK, 128)
-
-    def columns(piece):
-        return piece.transpose(1, 0, 2).reshape(piece.shape[1], HID)
-
-    return (
-        final.reshape(state.shape),
-        columns(blocks[:, 1024:1152]),
-        columns(blocks[:, :1024]),
-        columns(blocks[:, 1152:]).T,
-    )
+    anywhere = pl.BlockSpec(memory_space=pl.ANY)
+    field, first, middle, last = pl.pallas_call(
+        write_out,
+        out_shape=(
+            jax.ShapeDtypeStruct((ROWS, FEAT), F32),
+            jax.ShapeDtypeStruct((FEAT, HID), F32),
+            jax.ShapeDtypeStruct((HID, HID), F32),
+            jax.ShapeDtypeStruct((HID, FEAT), F32),
+        ),
+        in_specs=[vmem] * 2,
+        out_specs=(anywhere,) * 4,
+        scratch_shapes=[dma((25,))],
+        compiler_params=pltpu.CompilerParams(vmem_limit_bytes=8 * 1024 * 1024),
+        name="write_out",
+    )(final, total)
+    return field.reshape(state.shape), first, middle, last
 
 
 def solution(mesh):

time: 142 us -> 119 us (0.84)
  Pallas kernels: 131 us -> 119 us
  local copies, waits for them, and re-layouts: 10 us -> 0 us
    pallas_call x1 -> x2, Pallas kernels: 131 us -> 119 us  [the longest x1 116 us: body(): pl.pallas_call(kernel, out_shape=(pltpu.VMEM((ROWS, FEAT), F32), pltpu.VM...]
    reshape x2 -> x0, local copies, waits for them, and re-layouts: 5.68 us -> none  [columns(): return piece.transpose(1, 0, 2).reshape(piece.shape[1], HID)]
    transpose x2 -> x0, local copies, waits for them, and re-layouts: 2.27 us -> none  [columns(): return piece.transpose(1, 0, 2).reshape(piece.shape[1], HID)]
where the time goes in v2:
time: 119 us
  Pallas kernels  119 us (100%)
    pallas_call x1, Pallas kernels, body(): pl.pallas_call(kernel, out_shape=(pltpu.VMEM((ROWS, FEAT), F32), pltpu.VM...  116 us
    pallas_call x1, Pallas kernels, body(): pl.pallas_call(write_out, out_shape=(jax.ShapeDtypeStruct((ROWS, FEAT), F...  2.6 us

profile of v2, /device:TPU:1, one launch (start us, length us, event | category | flops | bytes accessed | tf_op | source)
XLA Modules:
  0.0 119.3 jit_solution(17404896173989939162)
XLA Ops:
  0.6 116.1 %spectral_steps.1 = (f32[512,128]{1,0:T(8,128)S(1)}, f32[10240,128]{1,0:T(8,128)S(1)}) custom-call(f32[512,128]{1,0:T(8,128)} %bitcast.3, f32[512,128]{1,0:T(8,128)} %bitcast.4, bf16[128,1024]{1,0:T(8,128)(2,1)} %w1_in.1, bf16[1024,1024]{1,0:T(8,128)(2,1)} %w2_in.1, bf16[1024,128]{1,0:T(8,128)(2,1)} %w3_in.1, f32[2360,128]{1,0:T(8,128)} %constant.8.clone.tab_in, ...), custom_call_target="tpu_custom_call" | custom-call | tf_op jit(solution)/shard_map/spectral_steps/pallas_call | solution.py:476
  116.7 2.6 %write_out.1 = (f32[512,128]{1,0:T(8,128)}, f32[128,1024]{1,0:T(8,128)}, f32[1024,1024]{1,0:T(8,128)}, f32[1024,128]{1,0:T(8,128)}) custom-call(f32[512,128]{1,0:T(8,128)S(1)} %get-tuple-element.10.final, f32[10240,128]{1,0:T(8,128)S(1)} %get-tuple-element.11.total), custom_call_target="tpu_custom_call" | custom-call | tf_op jit(solution)/shard_map/write_out/pallas_call | solution.py:504

commit v3 on v2

--- a/solution.py
+++ b/solution.py
@@ -106,7 +106,7 @@
     state_in, cot_in, w1_in, w2_in, w3_in, tab_in, tf_in, ti_in, quad_in,
     final, total,
     state, cot, w1, w2, w3, tab, tf, ti,
-    grads, field, x0, x1, gt, ha0, hb0, da0, db0, ha1, hb1, da1, db1, ga, gb,
+    inward, outward, grads, field, x0, x1, gt, ha0, hb0, da0, db0, ha1, hb1, da1, db1, ga, gb,
     send, recv, core_buf, half_buf, z_buf,
     loads, a2a_send, a2a_recv, core_send, core_recv, rs_send, rs_recv, z_send, z_recv,
 ):
@@ -166,38 +166,46 @@
         tend = jnp.dot(hb[rows, :], w3[...], preferred_element_type=F32)
         field[rows, :] = source[rows, :] + 0.5 * tend
 
-    def backward(lat, da, db, pulled, want_rows):
+    def backward_b(lat, db):
         rows = pl.ds(pl.multiple_of(lat * NLON, NLON), NLON)
         scaled = gt[rows, :]
         for n in range(4):
             cols = slice(n * 256, (n + 1) * 256)
             gb[rows, cols] = (nt(scaled, w3[cols, :]) * db[rows, cols]).astype(BF)
+
+    def backward_a(lat, da, pulled):
+        rows = pl.ds(pl.multiple_of(lat * NLON, NLON), NLON)
         grad_b = gb[rows, :]
         for n in range(4):
             cols = slice(n * 256, (n + 1) * 256)
             ga[rows, cols] = (nt(grad_b, w2[cols, :]) * da[rows, cols]).astype(BF)
-        if want_rows:
+        if pulled is not None:
             pulled[rows, :] = pulled[rows, :] + nt(ga[rows, :], w1[...])
 
-    def weight_grads(x, ha, hb, add):
-        def put(start, value, flip=False):
-            for half in range(2):
-                block = value[:, half * 128 : (half + 1) * 128]
-                block = block.T if flip else block
-                rows = pl.ds(pl.multiple_of(start + half * BLK, 128), block.shape[0])
-                grads[rows, :] = block + grads[rows, :] if add else block
-
-        def middle(i, carry):
+    def put(start, value, add, flip=False):
+        for half in range(2):
+            block = value[:, half * 128 : (half + 1) * 128]
+            block = block.T if flip else block
+            rows = pl.ds(pl.multiple_of(start + half * BLK, 128), block.shape[0])
+            grads[rows, :] = block + grads[rows, :] if add else block
+
+    def some(half, n):
+        return pl.ds(pl.multiple_of(half * 512 + n * 256, 256), 256)
+
+    def middle_grads(half, ha, add):
+        def run(i, carry):
             left = ha[:, pl.ds(pl.multiple_of(i * 256, 256), 256)]
-            for n in range(4):
-                put(2 * n * BLK + i * 256, tn(left, gb[:, n * 256 : (n + 1) * 256]))
+            for n in range(2):
+                put((half * 4 + 2 * n) * BLK + i * 256, tn(left, gb[:, some(half, n)]), add)
             return carry
 
-        lax.fori_loop(0, 4, middle, 0)
-        for n in range(4):
-            cols = slice(n * 256, (n + 1) * 256)
-            put(2 * n * BLK + 1024, tn(x[...], ga[:, cols]))
-            put(2 * n * BLK + 1152, tn(gt[...], hb[:, cols]), True)
+        lax.fori_loop(0, 4, run, 0)
+
+    def outer_grads(half, x, hb, add):
+        for n in range(2):
+            start = (half * 4 + 2 * n) * BLK
+            put(start + 1024, tn(x[...], ga[:, some(half, n)]), add)
+            put(start + 1152, tn(gt[...], hb[:, some(half, n)]), add, True)
 
     def lanes(ref):
         return jnp.concatenate([ref[0:NLON, :], ref[NLON : 2 * NLON, :]], axis=1)
@@ -216,19 +224,21 @@
         return ref.at[index, pl.ds(pl.multiple_of(device * 8, 8), 8), :].at[pl.ds(4 * kind, 4), :]
 
     def exchange(index, kind):
-        def start(j, carry):
-            target = lax.rem(me + 18 + j + j // 46, BANDS)
-            pltpu.make_async_remote_copy(
-                src_ref=piece(send, index, target, kind),
-                dst_ref=piece(recv, index, me, kind),
-                send_sem=a2a_send.at[2 * index + kind],
-                recv_sem=a2a_recv.at[2 * index + kind],
-                device_id={"lat": target, "dp": dp},
-                device_id_type=MESH,
-            ).start()
+        def start(i, carry):
+            for k in range(7):
+                j = i * 7 + k
+                target = lax.rem(me + 18 + j + j // 46, BANDS)
+                pltpu.make_async_remote_copy(
+                    src_ref=piece(send, index, target, kind),
+                    dst_ref=piece(recv, index, me, kind),
+                    send_sem=a2a_send.at[2 * index + kind],
+                    recv_sem=a2a_recv.at[2 * index + kind],
+                    device_id={"lat": target, "dp": dp},
+                    device_id_type=MESH,
+                ).start()
             return carry
 
-        lax.fori_loop(0, BANDS - 1, start, 0)
+        lax.fori_loop(0, 9, start, 0)
         mine = pl.ds(pl.multiple_of(me * 8, 8) + 4 * kind, 4)
         recv[index, mine, :] = send[index, mine, :]
 
@@ -238,11 +248,15 @@
             half = ref.at[index, most, :]
             pltpu.make_async_copy(half, half, sem.at[2 * index + kind]).wait()
 
-    def legendre(source, target, kind):
+    def legendre_tables():
         degree = me + lax.broadcasted_iota(jnp.int32, (MW, NLAT), 0)
         size = (degree * (degree + 1)).astype(F32)
         damping = jnp.where(degree <= MW - 1, 1.0 / (1.0 + size / (MW * (MW - 1.0))), 0.0)
         poly = tab[...]
+        inward[...] = terms(poly * damping)
+        outward[...] = terms(poly.T)
+
+    def legendre(source, target, kind):
         value = jnp.concatenate(
             [
                 jnp.concatenate(
@@ -253,8 +267,8 @@
             ],
             axis=1,
         )
-        coeffs = times(terms(poly * damping), value)
-        back = times(terms(poly.T), coeffs)
+        coeffs = times(inward[...], value)
+        back = times(outward[...], coeffs)
         for part in range(2):
             for lat in range(2):
                 target[pl.ds(kind * 4 + lat * 2 + part, BANDS, stride=8), :] = back[
@@ -280,21 +294,16 @@
         loading[name].wait()
     x0[...] = state[...].astype(BF)
 
-    def opening(lat):
-        forward(lat, x0, state, ha0, hb0, da0, db0)
-
-        @pl.when(lat == 0)
-        def _():
-            pl.semaphore_wait(barrier, BANDS + 1)
-            exchange(0, 1)
-
-    both(opening)
+    both(lambda lat: forward(lat, x0, state, ha0, hb0, da0, db0))
     to_waves(field, 0, send.at[0])
+    pl.semaphore_wait(barrier, BANDS + 1)
     exchange(0, 0)
+    exchange(0, 1)
     for name in ("ti", "tab"):
         loading[name].wait()
+    legendre_tables()
+    turn(0, 0)
     turn(0, 1)
-    turn(0, 0)
 
     halves = [(slice(lat * NLON, (lat + 1) * NLON), slice(lat * FEAT, (lat + 1) * FEAT)) for lat in range(2)]
     arrive(1, 0)
@@ -310,10 +319,13 @@
     for rows, cols in halves:
         final[rows, :] = pulled[:, cols]
         gt[rows, :] = (0.5 * pulled[:, cols]).astype(BF)
-    both(lambda lat: backward(lat, da1, db1, final, True))
+    both(lambda lat: backward_b(lat, db1))
+    both(lambda lat: backward_a(lat, da1, final))
     to_waves(final, 1, send.at[2])
     exchange(2, 1)
-    weight_grads(x1, ha1, hb1, False)
+    for half in range(2):
+        middle_grads(half, ha1, False)
+        outer_grads(half, x1, hb1, False)
     turn(2, 1)
     turn(2, 0)
 
@@ -321,8 +333,7 @@
     pulled = to_grid(recv.at[3], 1)
     for rows, cols in halves:
         gt[rows, :] = (0.5 * pulled[:, cols]).astype(BF)
-    both(lambda lat: backward(lat, da0, db0, None, False))
-    weight_grads(x0, ha0, hb0, True)
+    both(lambda lat: backward_b(lat, db0))
 
     def tiles(ref, start, count):
         return ref.at[pl.ds(pl.multiple_of(start * 8, 8), count * 8), :]
@@ -351,19 +362,42 @@
     )
     size = 80
     parts = range(8)
-    starts = []
-    for s in parts:
-        c = copy(
-            tiles(grads, (1 - core) * 640 + s * size, size), tiles(core_buf, s * size, size),
-            core_send.at[s], core_recv.at[s], mate,
-        )
-        c.start()
-        starts.append(c)
-    arrive(3, 0)
-    value = to_grid(recv.at[3], 0)
-    for rows, cols in halves:
-        final[rows, :] = value[:, cols]
+    starts = {}
+
+    def to_mate(chosen):
+        for s in chosen:
+            c = copy(
+                tiles(grads, (1 - core) * 640 + s * size, size), tiles(core_buf, s * size, size),
+                core_send.at[s], core_recv.at[s], mate,
+            )
+            c.start()
+            starts[s] = c
+
+    middle_grads(1 - core, ha0, True)
+    to_mate((0, 2, 4, 6))
+    both(lambda lat: backward_a(lat, da0, None))
+    outer_grads(1 - core, x0, hb0, True)
+    to_mate((1, 3, 5, 7))
+    middle_grads(core, ha0, True)
+    outer_grads(core, x0, hb0, True)
     offset = [core * 640 + s * size for s in parts]
+    def along_z(index):
+        return {"lat": xl * 32 + index * 4 + y, "dp": dp}
+
+    def to_owner(s, act):
+        @pl.when(z != s)
+        def _():
+            act(
+                copy(
+                    tiles(grads, kept[s][4], 5), tiles(z_buf, 5 * z, 5),
+                    z_send.at[s], z_recv.at[z], along_z(s),
+                )
+            )
+
+    def from_owner(index, i):
+        held = tiles(total, chunk(index), 5)
+        return copy(held, held, z_send.at[8 + i], z_recv.at[8 + index], along_z(lax.rem(z + i, 8)))
+
     kept = [[o] for o in offset]
     place = 0
     running = {}
@@ -378,6 +412,8 @@
                 c.wait()
                 add(keep, half_buf, base, size >> step)
                 kept[s].append(keep)
+            if step == 4:
+                to_owner(s, lambda c: c.start())
             if step < 4:
                 name = order[s % 4][step]
                 now = kept[s][step]
@@ -398,41 +434,35 @@
         return start
 
     own = chunk(z)
-    zs = []
-    for i in range(1, 8):
-        other = lax.rem(z + i, 8)
-        c = copy(
-            tiles(grads, chunk(other), 5), tiles(z_buf, 5 * (i - 1), 5),
-            z_send.at[i - 1], z_recv.at[i - 1], {"lat": xl * 32 + other * 4 + y, "dp": dp},
-        )
-        c.start()
-        zs.append(c)
-    for c in zs:
-        c.wait()
+    arrive(3, 0)
+    value = to_grid(recv.at[3], 0)
+    for rows, cols in halves:
+        final[rows, :] = value[:, cols]
+    others = [lax.rem(z + i, 8) for i in range(1, 8)]
+    for other in others:
+        copy(
+            tiles(grads, own, 5), tiles(z_buf, 5 * other, 5), z_send.at[0], z_recv.at[other], along_z(other)
+        ).wait_recv()
     for j in range(5):
         rows = pl.ds(pl.multiple_of((own + j) * 8, 8), 8)
         value = grads[rows, :]
-        for i in range(7):
-            value = value + z_buf[(5 * i + j) * 8 : (5 * i + j + 1) * 8, :]
+        for other in others:
+            value = value + z_buf[pl.ds(pl.multiple_of((5 * other + j) * 8, 8), 8), :]
         total[rows, :] = value
-
-    zs = []
     for i in range(1, 8):
-        other = lax.rem(z + i, 8)
-        c = copy(
-            tiles(total, own, 5), tiles(total, own, 5),
-            z_send.at[6 + i], z_recv.at[6 + i], {"lat": xl * 32 + other * 4 + y, "dp": dp},
-        )
-        c.start()
-        zs.append(c)
-    for c in zs:
-        c.wait()
+        from_owner(z, i).start()
     running = {}
     last = []
     for step in (3, 2, 1, 0, -1):
         for s in parts:
             if step < 3:
                 running[s].wait()
+            else:
+
+                @pl.when(z != s)
+                def _():
+                    from_owner(s, 1).wait_recv()
+
             if step >= 0:
                 count = size >> (step + 1)
                 held = tiles(total, kept[s][step + 1], count)
@@ -447,6 +477,10 @@
                 c = copy(held, held, core_send.at[8 + sem], core_recv.at[8 + sem], mate)
                 c.start()
                 last.append(c)
+    for s in parts:
+        to_owner(s, lambda c: c.wait_send())
+    for i in range(1, 8):
+        from_owner(z, i).wait_send()
     for c in last:
         c.wait()
 
@@ -485,12 +519,13 @@
             pltpu.VMEM((ROWS, FEAT), F32), pltpu.VMEM((ROWS, FEAT), F32),
             pltpu.VMEM((FEAT, HID), BF), pltpu.VMEM((HID, HID), BF), pltpu.VMEM((HID, FEAT), BF),
             pltpu.VMEM((MW, NLAT), F32), pltpu.VMEM(to_waves.shape, BF), pltpu.VMEM(to_grid.shape, BF),
+            pltpu.VMEM((MW, 3 * NLAT), BF), pltpu.VMEM((NLAT, 3 * MW), BF),
             pltpu.VMEM((8 * BLK, 128), F32), pltpu.VMEM((ROWS, FEAT), F32), thin, thin, thin,
             act, act, slope, slope, act, act, slope, slope, act, act,
             pltpu.VMEM((4, 8 * BANDS, FEAT), F32), pltpu.VMEM((4, 8 * BANDS, FEAT), F32),
             pltpu.VMEM((640 * 8, 128), F32), pltpu.VMEM((600 * 8, 128), F32),
-            pltpu.VMEM((35 * 8, 128), F32),
-            dma((8,)), dma((8,)), dma((8,)), dma((32,)), dma((32,)), dma((64,)), dma((64,)), dma((14,)), dma((14,)),
+            pltpu.VMEM((40 * 8, 128), F32),
+            dma((8,)), dma((8,)), dma((8,)), dma((32,)), dma((32,)), dma((64,)), dma((64,)), dma((16,)), dma((16,)),
         ],
         compiler_params=pltpu.CompilerParams(
             collective_id=0, has_side_effects=True, vmem_limit_bytes=57 * 1024 * 1024

time: 119 us -> 113 us (0.950)
  Pallas kernels: 119 us -> 112 us
    pallas_call x1, Pallas kernels: 116 us -> 110 us  [body(): pl.pallas_call(kernel, out_shape=(pltpu.VMEM((ROWS, FEAT), F32), pltpu.VM...]
where the time goes in v3:
time: 113 us
  Pallas kernels  112 us (99%)
    pallas_call x1, Pallas kernels, body(): pl.pallas_call(kernel, out_shape=(pltpu.VMEM((ROWS, FEAT), F32), pltpu.VM...  110 us
    pallas_call x1, Pallas kernels, body(): pl.pallas_call(write_out, out_shape=(jax.ShapeDtypeStruct((ROWS, FEAT), F...  2.6 us

profile of v3, /device:TPU:1, one launch (start us, length us, event | category | flops | bytes accessed | tf_op | source)
XLA Modules:
  0.0 112.9 jit_solution(17296172753080184262)
XLA Ops:
  0.6 109.7 %spectral_steps.1 = (f32[512,128]{1,0:T(8,128)S(1)}, f32[10240,128]{1,0:T(8,128)S(1)}) custom-call(f32[512,128]{1,0:T(8,128)} %bitcast.3, f32[512,128]{1,0:T(8,128)} %bitcast.4, bf16[128,1024]{1,0:T(8,128)(2,1)} %w1_in.1, bf16[1024,1024]{1,0:T(8,128)(2,1)} %w2_in.1, bf16[1024,128]{1,0:T(8,128)(2,1)} %w3_in.1, f32[2360,128]{1,0:T(8,128)} %constant.8.clone.tab_in, ...), custom_call_target="tpu_custom_call" | custom-call | tf_op jit(solution)/shard_map/spectral_steps/pallas_call | solution.py:510
  110.3 2.6 %write_out.1 = (f32[512,128]{1,0:T(8,128)}, f32[128,1024]{1,0:T(8,128)}, f32[1024,1024]{1,0:T(8,128)}, f32[1024,128]{1,0:T(8,128)}) custom-call(f32[512,128]{1,0:T(8,128)S(1)} %get-tuple-element.10.final, f32[10240,128]{1,0:T(8,128)S(1)} %get-tuple-element.11.total), custom_call_target="tpu_custom_call" | custom-call | tf_op jit(solution)/shard_map/write_out/pallas_call | solution.py:539

commit v4 on v3

--- a/solution.py
+++ b/solution.py
@@ -125,6 +125,28 @@
     }
     bit = {"xa": lax.rem(xl + xh, 2), "xb": xh, "ya": lax.rem(yl + yh, 2), "yb": yh}
 
+    def partners(act):
+        def run(first, width):
+            def inner(i, carry):
+                for k in range(width):
+                    act(lax.rem(me + (first + i * width + k), BANDS))
+                return carry
+
+            return inner
+
+        lax.fori_loop(0, 4, run(44, 5), 0)
+        lax.fori_loop(0, 6, run(1, 7), 0)
+        act(lax.rem(me + 43, BANDS))
+
+    barrier = pltpu.get_barrier_semaphore()
+    partners(
+        lambda target: pl.semaphore_signal(
+            barrier, inc=1, device_id={"lat": target, "dp": dp}, device_id_type=MESH
+        )
+    )
+    for other in (mate, partner["xb"]):
+        pl.semaphore_signal(barrier, inc=1, device_id=other, device_id_type=MESH)
+
     group = me // 8
     first_row = 64 * (8 * group - group * (group - 1) // 2) + lax.rem(me, 8) * (8 - group) * 8
     wanted = {
@@ -137,18 +159,6 @@
     }
     for c in loading.values():
         c.start()
-
-    barrier = pltpu.get_barrier_semaphore()
-
-    def greet(j, carry):
-        pl.semaphore_signal(
-            barrier, inc=1, device_id={"lat": lax.rem(me + j, BANDS), "dp": dp}, device_id_type=MESH
-        )
-        return carry
-
-    lax.fori_loop(1, BANDS, greet, 0)
-    for other in (mate, partner["xb"]):
-        pl.semaphore_signal(barrier, inc=1, device_id=other, device_id_type=MESH)
 
     def forward(lat, x, source, ha, hb, da, db):
         rows = pl.ds(pl.multiple_of(lat * NLON, NLON), NLON)
@@ -224,21 +234,17 @@
         return ref.at[index, pl.ds(pl.multiple_of(device * 8, 8), 8), :].at[pl.ds(4 * kind, 4), :]
 
     def exchange(index, kind):
-        def start(i, carry):
-            for k in range(7):
-                j = i * 7 + k
-                target = lax.rem(me + 18 + j + j // 46, BANDS)
-                pltpu.make_async_remote_copy(
-                    src_ref=piece(send, index, target, kind),
-                    dst_ref=piece(recv, index, me, kind),
-                    send_sem=a2a_send.at[2 * index + kind],
-                    recv_sem=a2a_recv.at[2 * index + kind],
-                    device_id={"lat": target, "dp": dp},
-                    device_id_type=MESH,
-                ).start()
-            return carry
-
-        lax.fori_loop(0, 9, start, 0)
+        def start(target):
+            pltpu.make_async_remote_copy(
+                src_ref=piece(send, index, target, kind),
+                dst_ref=piece(recv, index, me, kind),
+                send_sem=a2a_send.at[2 * index + kind],
+                recv_sem=a2a_recv.at[2 * index + kind],
+                device_id={"lat": target, "dp": dp},
+                device_id_type=MESH,
+            ).start()
+
+        partners(start)
         mine = pl.ds(pl.multiple_of(me * 8, 8) + 4 * kind, 4)
         recv[index, mine, :] = send[index, mine, :]
 
@@ -312,8 +318,6 @@
         field[rows, :] = value[:, cols]
         x1[rows, :] = value[:, cols].astype(BF)
     both(lambda lat: forward(lat, x1, field, ha1, hb1, da1, db1))
-    to_waves(field, 0, send.at[2])
-    exchange(2, 0)
     arrive(1, 1)
     pulled = to_grid(recv.at[1], 1)
     for rows, cols in halves:
@@ -323,6 +327,8 @@
     both(lambda lat: backward_a(lat, da1, final))
     to_waves(final, 1, send.at[2])
     exchange(2, 1)
+    to_waves(field, 0, send.at[2])
+    exchange(2, 0)
     for half in range(2):
         middle_grads(half, ha1, False)
         outer_grads(half, x1, hb1, False)
@@ -361,7 +367,7 @@
         ("yb", "ya", "xb", "xa"),
     )
     size = 80
-    parts = range(8)
+    parts = (0, 2, 4, 6, 1, 3, 5, 7)
     starts = {}
 
     def to_mate(chosen):
@@ -373,14 +379,49 @@
             c.start()
             starts[s] = c
 
-    middle_grads(1 - core, ha0, True)
-    to_mate((0, 2, 4, 6))
-    both(lambda lat: backward_a(lat, da0, None))
-    outer_grads(1 - core, x0, hb0, True)
-    to_mate((1, 3, 5, 7))
-    middle_grads(core, ha0, True)
-    outer_grads(core, x0, hb0, True)
-    offset = [core * 640 + s * size for s in parts]
+    offset = {s: core * 640 + s * size for s in parts}
+    kept = {s: [offset[s]] for s in parts}
+    place = 0
+    early, late = {}, {}
+
+    def take(entry):
+        c, start, base, count = entry
+        c.wait()
+        add(start, half_buf, base, count)
+
+    def reduce_step(s, step):
+        nonlocal place
+        count = size >> (step + 1)
+        now = kept[s][step]
+        if step >= 2:
+            take(late[s, step - 2])
+        if step == 0:
+            starts[s].wait()
+            add(offset[s], core_buf, s * size, size)
+        else:
+            take(early[s, step - 1])
+        if step == 4:
+            to_owner(s, lambda c: c.start())
+            return
+        name = order[s // 2][step]
+        keep = now + bit[name] * count
+        gone = now + (1 - bit[name]) * count
+        kept[s].append(keep)
+        if step == 3:
+            pieces = [(early, 0, count)]
+        else:
+            ahead = bit[order[s // 2][step + 1]]
+            pieces = [(early, (1 - ahead) * (count // 2), count // 2), (late, ahead * (count // 2), count // 2)]
+        for i, (book, at, length) in enumerate(pieces):
+            sem = 64 * i + step * 8 + s
+            c = copy(
+                tiles(grads, gone + at, length), tiles(half_buf, place, length),
+                rs_send.at[sem], rs_recv.at[sem], partner[name],
+            )
+            c.start()
+            book[s, step] = (c, keep + at, place, length)
+            place += length
+
     def along_z(index):
         return {"lat": xl * 32 + index * 4 + y, "dp": dp}
 
@@ -398,34 +439,20 @@
         held = tiles(total, chunk(index), 5)
         return copy(held, held, z_send.at[8 + i], z_recv.at[8 + index], along_z(lax.rem(z + i, 8)))
 
-    kept = [[o] for o in offset]
-    place = 0
-    running = {}
-    for step in range(5):
-        count = size >> (step + 1)
+    middle_grads(1 - core, ha0, True)
+    to_mate(parts[:4])
+    middle_grads(core, ha0, True)
+    both(lambda lat: backward_a(lat, da0, None))
+    for s in parts[:4]:
+        reduce_step(s, 0)
+    outer_grads(1 - core, x0, hb0, True)
+    to_mate(parts[4:])
+    outer_grads(core, x0, hb0, True)
+    for s in parts[4:]:
+        reduce_step(s, 0)
+    for step in range(1, 5):
         for s in parts:
-            if step == 0:
-                starts[s].wait()
-                add(offset[s], core_buf, s * size, size)
-            else:
-                c, keep, base = running[s]
-                c.wait()
-                add(keep, half_buf, base, size >> step)
-                kept[s].append(keep)
-            if step == 4:
-                to_owner(s, lambda c: c.start())
-            if step < 4:
-                name = order[s % 4][step]
-                now = kept[s][step]
-                keep = now + bit[name] * count
-                gone = now + (1 - bit[name]) * count
-                c = copy(
-                    tiles(grads, gone, count), tiles(half_buf, place, count),
-                    rs_send.at[step * 8 + s], rs_recv.at[step * 8 + s], partner[name],
-                )
-                c.start()
-                running[s] = (c, keep, place)
-                place += count
+            reduce_step(s, step)
 
     def chunk(index):
         start = kept[7][4]
@@ -451,25 +478,33 @@
         total[rows, :] = value
     for i in range(1, 8):
         from_owner(z, i).start()
-    running = {}
+    running = {s: [] for s in parts}
     last = []
+
+    def pass_on(s, step, start, length, sem):
+        held = tiles(total, start, length)
+        c = copy(held, held, rs_send.at[sem], rs_recv.at[sem], partner[order[s // 2][step]])
+        c.start()
+        running[s].append((step, c))
+
     for step in (3, 2, 1, 0, -1):
         for s in parts:
             if step < 3:
-                running[s].wait()
+                for c in [c for at, c in running[s] if at == step + 1]:
+                    c.wait()
             else:
 
                 @pl.when(z != s)
                 def _():
                     from_owner(s, 1).wait_recv()
 
-            if step >= 0:
-                count = size >> (step + 1)
-                held = tiles(total, kept[s][step + 1], count)
-                sem = 32 + step * 8 + s
-                c = copy(held, held, rs_send.at[sem], rs_recv.at[sem], partner[order[s % 4][step]])
-                c.start()
-                running[s] = c
+            if step == 3:
+                pass_on(s, 3, kept[s][4], 5, 56 + s)
+            elif step >= 0:
+                half = size >> (step + 2)
+                pass_on(s, step, 2 * kept[s][step + 1] + half - kept[s][step + 2], half, 32 + step * 8 + s)
+            if step >= 1:
+                pass_on(s, step - 1, kept[s][step + 1], size >> (step + 1), 88 + (step - 1) * 8 + s)
             if step <= 0:
                 first = kept[s][1] if step == 0 else 2 * kept[s][0] + size // 2 - kept[s][1]
                 held = tiles(total, first, size // 2)
@@ -525,7 +560,7 @@
             pltpu.VMEM((4, 8 * BANDS, FEAT), F32), pltpu.VMEM((4, 8 * BANDS, FEAT), F32),
             pltpu.VMEM((640 * 8, 128), F32), pltpu.VMEM((600 * 8, 128), F32),
             pltpu.VMEM((40 * 8, 128), F32),
-            dma((8,)), dma((8,)), dma((8,)), dma((32,)), dma((32,)), dma((64,)), dma((64,)), dma((16,)), dma((16,)),
+            dma((8,)), dma((8,)), dma((8,)), dma((32,)), dma((32,)), dma((112,)), dma((112,)), dma((16,)), dma((16,)),
         ],
         compiler_params=pltpu.CompilerParams(
             collective_id=0, has_side_effects=True, vmem_limit_bytes=57 * 1024 * 1024

time: 113 us -> 109 us (0.965)
  Pallas kernels: 112 us -> 108 us
    pallas_call x1, Pallas kernels: 110 us -> 106 us  [body(): pl.pallas_call(kernel, out_shape=(pltpu.VMEM((ROWS, FEAT), F32), pltpu.VM...]
where the time goes in v4:
time: 109 us
  Pallas kernels  108 us (99%)
    pallas_call x1, Pallas kernels, body(): pl.pallas_call(kernel, out_shape=(pltpu.VMEM((ROWS, FEAT), F32), pltpu.VM...  106 us
    pallas_call x1, Pallas kernels, body(): pl.pallas_call(write_out, out_shape=(jax.ShapeDtypeStruct((ROWS, FEAT), F...  2.6 us

profile of v4, /device:TPU:1, one launch (start us, length us, event | category | flops | bytes accessed | tf_op | source)
XLA Modules:
  0.0 109.1 jit_solution(15092094000467676463)
XLA Ops:
  0.6 105.9 %spectral_steps.1 = (f32[512,128]{1,0:T(8,128)S(1)}, f32[10240,128]{1,0:T(8,128)S(1)}) custom-call(f32[512,128]{1,0:T(8,128)} %bitcast.3, f32[512,128]{1,0:T(8,128)} %bitcast.4, bf16[128,1024]{1,0:T(8,128)(2,1)} %w1_in.1, bf16[1024,1024]{1,0:T(8,128)(2,1)} %w2_in.1, bf16[1024,128]{1,0:T(8,128)(2,1)} %w3_in.1, f32[2360,128]{1,0:T(8,128)} %constant.8.clone.tab_in, ...), custom_call_target="tpu_custom_call" | custom-call | tf_op jit(solution)/shard_map/spectral_steps/pallas_call | solution.py:545
  106.5 2.6 %write_out.1 = (f32[512,128]{1,0:T(8,128)}, f32[128,1024]{1,0:T(8,128)}, f32[1024,1024]{1,0:T(8,128)}, f32[1024,128]{1,0:T(8,128)}) custom-call(f32[512,128]{1,0:T(8,128)S(1)} %get-tuple-element.10.final, f32[10240,128]{1,0:T(8,128)S(1)} %get-tuple-element.11.total), custom_call_target="tpu_custom_call" | custom-call | tf_op jit(solution)/shard_map/write_out/pallas_call | solution.py:574

commit v5 on v4

--- a/solution.py
+++ b/solution.py
@@ -160,7 +160,7 @@
     for c in loading.values():
         c.start()
 
-    def forward(lat, x, source, ha, hb, da, db):
+    def hidden(lat, x, ha, hb, da, db):
         rows = pl.ds(pl.multiple_of(lat * NLON, NLON), NLON)
         mine = x[rows, :]
         for layer in range(2):
@@ -173,6 +173,9 @@
                 out = pre * gate
                 act[rows, cols] = out.astype(BF)
                 slope[rows, cols] = gate * (1.0 + pre * (1.0 - gate))
+
+    def tendency(lat, source, hb):
+        rows = pl.ds(pl.multiple_of(lat * NLON, NLON), NLON)
         tend = jnp.dot(hb[rows, :], w3[...], preferred_element_type=F32)
         field[rows, :] = source[rows, :] + 0.5 * tend
 
@@ -248,11 +251,12 @@
         mine = pl.ds(pl.multiple_of(me * 8, 8) + 4 * kind, 4)
         recv[index, mine, :] = send[index, mine, :]
 
+    def bytes_of_all(ref, sem, index, kind):
+        half = ref.at[index, pl.ds(0, 4 * (BANDS - 1)), :]
+        pltpu.make_async_copy(half, half, sem.at[2 * index + kind]).wait()
+
     def arrive(index, kind):
-        most = pl.ds(0, 4 * (BANDS - 1))
-        for ref, sem in ((recv, a2a_recv), (send, a2a_send)):
-            half = ref.at[index, most, :]
-            pltpu.make_async_copy(half, half, sem.at[2 * index + kind]).wait()
+        bytes_of_all(recv, a2a_recv, index, kind)
 
     def legendre_tables():
         degree = me + lax.broadcasted_iota(jnp.int32, (MW, NLAT), 0)
@@ -300,7 +304,8 @@
         loading[name].wait()
     x0[...] = state[...].astype(BF)
 
-    both(lambda lat: forward(lat, x0, state, ha0, hb0, da0, db0))
+    both(lambda lat: hidden(lat, x0, ha0, hb0, da0, db0))
+    both(lambda lat: tendency(lat, state, hb0))
     to_waves(field, 0, send.at[0])
     pl.semaphore_wait(barrier, BANDS + 1)
     exchange(0, 0)
@@ -317,7 +322,7 @@
     for rows, cols in halves:
         field[rows, :] = value[:, cols]
         x1[rows, :] = value[:, cols].astype(BF)
-    both(lambda lat: forward(lat, x1, field, ha1, hb1, da1, db1))
+    both(lambda lat: hidden(lat, x1, ha1, hb1, da1, db1))
     arrive(1, 1)
     pulled = to_grid(recv.at[1], 1)
     for rows, cols in halves:
@@ -327,6 +332,7 @@
     both(lambda lat: backward_a(lat, da1, final))
     to_waves(final, 1, send.at[2])
     exchange(2, 1)
+    both(lambda lat: tendency(lat, field, hb1))
     to_waves(field, 0, send.at[2])
     exchange(2, 0)
     for half in range(2):
@@ -345,14 +351,19 @@
         return ref.at[pl.ds(pl.multiple_of(start * 8, 8), count * 8), :]
 
     def add(start, source, source_start, count):
+        width = 20 if count % 20 == 0 else 10 if count % 10 == 0 else 5
+
         def one(i, carry):
-            for j in range(5):
-                into = pl.ds(pl.multiple_of((start + i * 5 + j) * 8, 8), 8)
-                rows = pl.ds(pl.multiple_of((source_start + i * 5 + j) * 8, 8), 8)
+            for j in range(width):
+                into = pl.ds(pl.multiple_of((start + i * width + j) * 8, 8), 8)
+                rows = pl.ds(pl.multiple_of((source_start + i * width + j) * 8, 8), 8)
                 grads[into, :] = grads[into, :] + source[rows, :]
             return carry
 
-        lax.fori_loop(0, count // 5, one, 0)
+        if count == width:
+            one(0, 0)
+        else:
+            lax.fori_loop(0, count // width, one, 0)
 
     def copy(source, target, send_sem, recv_sem, device):
         return pltpu.make_async_remote_copy(
@@ -386,7 +397,7 @@
 
     def take(entry):
         c, start, base, count = entry
-        c.wait()
+        c.wait_recv()
         add(start, half_buf, base, count)
 
     def reduce_step(s, step):
@@ -396,8 +407,7 @@
         if step >= 2:
             take(late[s, step - 2])
         if step == 0:
-            starts[s].wait()
-            add(offset[s], core_buf, s * size, size)
+            starts[s].wait_recv()
         else:
             take(early[s, step - 1])
         if step == 4:
@@ -407,6 +417,8 @@
         keep = now + bit[name] * count
         gone = now + (1 - bit[name]) * count
         kept[s].append(keep)
+        if step == 0:
+            add(gone, core_buf, s * size + (1 - bit[name]) * count, count)
         if step == 3:
             pieces = [(early, 0, count)]
         else:
@@ -421,6 +433,8 @@
             c.start()
             book[s, step] = (c, keep + at, place, length)
             place += length
+        if step == 0:
+            add(keep, core_buf, s * size + bit[name] * count, count)
 
     def along_z(index):
         return {"lat": xl * 32 + index * 4 + y, "dp": dp}
@@ -491,7 +505,7 @@
         for s in parts:
             if step < 3:
                 for c in [c for at, c in running[s] if at == step + 1]:
-                    c.wait()
+                    c.wait_recv()
             else:
 
                 @pl.when(z != s)
@@ -517,7 +531,15 @@
     for i in range(1, 8):
         from_owner(z, i).wait_send()
     for c in last:
-        c.wait()
+        c.wait_recv()
+    for index in range(4):
+        for kind in range(2):
+            bytes_of_all(send, a2a_send, index, kind)
+    for c in [*starts.values(), *[entry[0] for entry in [*early.values(), *late.values()]], *last]:
+        c.wait_send()
+    for s in parts:
+        for _, c in running[s]:
+            c.wait_send()
 
 
 def write_out(final, total, field, first, middle, last, sems):

time: 109 us -> 108 us (level)
  no operation moved by 1% of the time
where the time goes in v5:
time: 108 us
  Pallas kernels  108 us (100%)
    pallas_call x1, Pallas kernels, body(): pl.pallas_call(kernel, out_shape=(pltpu.VMEM((ROWS, FEAT), F32), pltpu.VM...  105 us
    pallas_call x1, Pallas kernels, body(): pl.pallas_call(write_out, out_shape=(jax.ShapeDtypeStruct((ROWS, FEAT), F...  2.6 us

profile of v5, /device:TPU:1, one launch (start us, length us, event | category | flops | bytes accessed | tf_op | source)
XLA Modules:
  0.0 108.3 jit_solution(4632661460934698464)
XLA Ops:
  0.6 105.0 %spectral_steps.1 = (f32[512,128]{1,0:T(8,128)S(1)}, f32[10240,128]{1,0:T(8,128)S(1)}) custom-call(f32[512,128]{1,0:T(8,128)} %bitcast.3, f32[512,128]{1,0:T(8,128)} %bitcast.4, bf16[128,1024]{1,0:T(8,128)(2,1)} %w1_in.1, bf16[1024,1024]{1,0:T(8,128)(2,1)} %w2_in.1, bf16[1024,128]{1,0:T(8,128)(2,1)} %w3_in.1, f32[2360,128]{1,0:T(8,128)} %constant.8.clone.tab_in, ...), custom_call_target="tpu_custom_call" | custom-call | tf_op jit(solution)/shard_map/spectral_steps/pallas_call | solution.py:567
  105.7 2.6 %write_out.1 = (f32[512,128]{1,0:T(8,128)}, f32[128,1024]{1,0:T(8,128)}, f32[1024,1024]{1,0:T(8,128)}, f32[1024,128]{1,0:T(8,128)}) custom-call(f32[512,128]{1,0:T(8,128)S(1)} %get-tuple-element.10.final, f32[10240,128]{1,0:T(8,128)S(1)} %get-tuple-element.11.total), custom_call_target="tpu_custom_call" | custom-call | tf_op jit(solution)/shard_map/write_out/pallas_call | solution.py:596

commit v6 on v5

--- a/solution.py
+++ b/solution.py
@@ -501,7 +501,13 @@
         c.start()
         running[s].append((step, c))
 
-    for step in (3, 2, 1, 0, -1):
+    def to_other_core(start, length, sem):
+        held = tiles(total, start, length)
+        c = copy(held, held, core_send.at[sem], core_recv.at[sem], mate)
+        c.start()
+        last.append(c)
+
+    for step in (3, 2, 1, 0):
         for s in parts:
             if step < 3:
                 for c in [c for at, c in running[s] if at == step + 1]:
@@ -519,13 +525,16 @@
                 pass_on(s, step, 2 * kept[s][step + 1] + half - kept[s][step + 2], half, 32 + step * 8 + s)
             if step >= 1:
                 pass_on(s, step - 1, kept[s][step + 1], size >> (step + 1), 88 + (step - 1) * 8 + s)
-            if step <= 0:
-                first = kept[s][1] if step == 0 else 2 * kept[s][0] + size // 2 - kept[s][1]
-                held = tiles(total, first, size // 2)
-                sem = 16 + 8 * step + s
-                c = copy(held, held, core_send.at[8 + sem], core_recv.at[8 + sem], mate)
-                c.start()
-                last.append(c)
+            if step == 0:
+                to_other_core(kept[s][1], size // 2, 16 + s)
+
+    for i in range(2):
+        for s in parts:
+            [c for at, c in running[s] if at == 0][i].wait_recv()
+            other = 2 * kept[s][0] + size // 2 - kept[s][1]
+            ahead = kept[s][2] - kept[s][1]
+            at = other + (ahead if i == 0 else size // 4 - ahead)
+            to_other_core(at, size // 4, 24 + 8 * i + s)
     for s in parts:
         to_owner(s, lambda c: c.wait_send())
     for i in range(1, 8):
@@ -582,7 +591,7 @@
             pltpu.VMEM((4, 8 * BANDS, FEAT), F32), pltpu.VMEM((4, 8 * BANDS, FEAT), F32),
             pltpu.VMEM((640 * 8, 128), F32), pltpu.VMEM((600 * 8, 128), F32),
             pltpu.VMEM((40 * 8, 128), F32),
-            dma((8,)), dma((8,)), dma((8,)), dma((32,)), dma((32,)), dma((112,)), dma((112,)), dma((16,)), dma((16,)),
+            dma((8,)), dma((8,)), dma((8,)), dma((40,)), dma((40,)), dma((112,)), dma((112,)), dma((16,)), dma((16,)),
         ],
         compiler_params=pltpu.CompilerParams(
             collective_id=0, has_side_effects=True, vmem_limit_bytes=57 * 1024 * 1024

time: 108 us -> 108 us (level)
  no operation moved by 1% of the time
where the time goes in v6:
time: 108 us
  Pallas kernels  108 us (100%)
    pallas_call x1, Pallas kernels, body(): pl.pallas_call(kernel, out_shape=(pltpu.VMEM((ROWS, FEAT), F32), pltpu.VM...  105 us
    pallas_call x1, Pallas kernels, body(): pl.pallas_call(write_out, out_shape=(jax.ShapeDtypeStruct((ROWS, FEAT), F...  2.6 us

profile of v6, /device:TPU:1, one launch (start us, length us, event | category | flops | bytes accessed | tf_op | source)
XLA Modules:
  0.0 108.3 jit_solution(9500589968172761057)
XLA Ops:
  0.6 105.1 %spectral_steps.1 = (f32[512,128]{1,0:T(8,128)S(1)}, f32[10240,128]{1,0:T(8,128)S(1)}) custom-call(f32[512,128]{1,0:T(8,128)} %bitcast.3, f32[512,128]{1,0:T(8,128)} %bitcast.4, bf16[128,1024]{1,0:T(8,128)(2,1)} %w1_in.1, bf16[1024,1024]{1,0:T(8,128)(2,1)} %w2_in.1, bf16[1024,128]{1,0:T(8,128)(2,1)} %w3_in.1, f32[2360,128]{1,0:T(8,128)} %constant.8.clone.tab_in, ...), custom_call_target="tpu_custom_call" | custom-call | tf_op jit(solution)/shard_map/spectral_steps/pallas_call | solution.py:576
  105.7 2.6 %write_out.1 = (f32[512,128]{1,0:T(8,128)}, f32[128,1024]{1,0:T(8,128)}, f32[1024,1024]{1,0:T(8,128)}, f32[1024,128]{1,0:T(8,128)}) custom-call(f32[512,128]{1,0:T(8,128)S(1)} %get-tuple-element.10.final, f32[10240,128]{1,0:T(8,128)S(1)} %get-tuple-element.11.total), custom_call_target="tpu_custom_call" | custom-call | tf_op jit(solution)/shard_map/write_out/pallas_call | solution.py:605
